TPU v7x, 32 devices: a 4x4x1 block of a 4x4x8 slice. The times are simulated.
32 devices in a mesh: dp: 1 (over z), tp: 32 (over y, x, core).
Axes of the slice: x: 4, y: 4, z: 1, core: 2. Of those that a mesh axis runs over, the one named last changes fastest.
The devices are a block of a 4x4x8 slice.
Arguments:
- queries: bfloat16 [8192, 384], P(('dp', 'tp'))
- w_first: bfloat16 [384, 1536], replicated
- w_second: bfloat16 [1536, 384], replicated
- catalogue: bfloat16 [65536, 384], P('tp')
- log_q: float32 [65536], P('tp')
- labels: int32 [8192], P(('dp', 'tp'))
Outputs:
- output 1: float32 [1], P('dp')
- output 2: bfloat16 [65536, 384], P(('dp', 'tp'))
- output 3: bfloat16 [384, 1536], P('dp')
- output 4: bfloat16 [1536, 384], P('dp')
All inputs are finite; a program needn't handle non-finite values.
Results may differ from a plain program's by a relative error of at most 0.00366648.
Values are sent between devices in bfloat16 or wider.
A program may use at most 768 MiB of HBM per device.

v0:
```python
import jax
import jax.numpy as jnp
from jax import lax
from jax.sharding import PartitionSpec as P


def solution(mesh):
    def local_step(queries, w_first, w_second, catalogue, log_q, labels):
        items_local = catalogue.shape[0]
        shard_index = lax.axis_index("tp")
        pre_act = jnp.dot(queries, w_first, preferred_element_type=jnp.float32)
        hidden = jnp.maximum(pre_act, 0.0).astype(jnp.bfloat16)
        query_emb = jnp.dot(hidden, w_second, preferred_element_type=jnp.float32).astype(jnp.bfloat16)
        emb_all = lax.all_gather(query_emb, "tp", axis=0, tiled=True)
        labels_all = lax.all_gather(labels, "tp", axis=0, tiled=True)
        total_rows = emb_all.shape[0]
        logits = lax.dot_general(emb_all, catalogue, (((1,), (1,)), ((), ())), preferred_element_type=jnp.float32) - log_q[None, :]
        local_max = jnp.max(logits, axis=1)
        local_ids = labels_all - shard_index * items_local
        label_hit = lax.broadcasted_iota(jnp.int32, (1, items_local), 1) == local_ids[:, None]
        local_target = jnp.sum(jnp.where(label_hit, logits, 0.0), axis=1)
        exp_local = jnp.exp(logits - local_max[:, None])
        local_sum = jnp.sum(exp_local, axis=1)
        row_max = lax.pmax(local_max, "tp")
        rescale = jnp.exp(local_max - row_max)
        row_stats = lax.psum(jnp.stack([local_sum * rescale, local_target]), "tp")
        sum_exp = row_stats[0]
        mean_loss = jnp.mean(row_max + jnp.log(sum_exp) - row_stats[1]).reshape(1)
        soft_prob = exp_local * (rescale / sum_exp)[:, None]
        grad_logits = (jnp.where(label_hit, soft_prob - 1.0, soft_prob) / total_rows).astype(jnp.bfloat16)
        grad_items = lax.dot_general(grad_logits, emb_all, (((0,), (0,)), ((), ())), preferred_element_type=jnp.float32).astype(jnp.bfloat16)
        emb_part = jnp.dot(grad_logits, catalogue, preferred_element_type=jnp.float32)
        grad_emb = lax.psum_scatter(emb_part, "tp", scatter_dimension=0, tiled=True).astype(jnp.bfloat16)
        second_part = lax.dot_general(hidden, grad_emb, (((0,), (0,)), ((), ())), preferred_element_type=jnp.float32)
        grad_hidden = lax.dot_general(grad_emb, w_second, (((1,), (1,)), ((), ())), preferred_element_type=jnp.float32)
        grad_pre = jnp.where(pre_act > 0.0, grad_hidden, 0.0).astype(jnp.bfloat16)
        first_part = lax.dot_general(queries, grad_pre, (((0,), (0,)), ((), ())), preferred_element_type=jnp.float32)
        grad_first, grad_second = lax.psum((first_part, second_part), "tp")
        return mean_loss, grad_items, grad_first.astype(jnp.bfloat16), grad_second.astype(jnp.bfloat16)

    row_spec = P(("dp", "tp"), None)
    return jax.shard_map(local_step, mesh=mesh, in_specs=(row_spec, P(None, None), P(None, None), P("tp", None), P("tp"), P(("dp", "tp"))), out_specs=(P("dp"), row_spec, P("dp", None), P("dp", None)), check_vma=False)
```

profile of v0, /device:TPU:97, one launch (start us, length us, event | category | flops | bytes accessed | tf_op | source)
XLA Modules:
  0.0 499.9 jit_solution(10967902803689587286)
XLA Ops:
  7.2 0.1 all-gather.3.cloned.1.call-start
  7.3 2.0 fusion.15
  9.3 2.5 convolution_convert_fusion.1
  11.8 0.1 all-gather.3.cloned.1.call-update
  11.9 0.1 all-reduce.4.cloned.1.call-start
  12.0 31.7 %all-gather = s32[32,1,256]{2,1,0:T(1,128)S(1)} all-gather(s32[1,1,256]{2,1,0:T(1,128)} %bitcast.29), channel_id=1, replica_groups=mesh['dp'=1,'tp'=32] {'tp'}, dimensions={0}, use_global_device_ids=true | all-gather | bytes 33792 | tf_op jit(solution)/shard_map/all_gather | solution.py:15
  43.7 16.5 %all-gather.3.cloned.1.call-done = bf16[8192,384]{1,0:T(8,128)(2,1)} async-done(((bf16[256,384]{1,0:T(8,128)(2,1)}), bf16[8192,384]{1,0:T(8,128)(2,1)}) %all-gather.3.cloned.1.call-update) | async-done | bytes 6291472 | tf_op jit(solution)/shard_map/all_gather | solution.py:14
  60.2 28.3 %subtract_reduce_fusion = (f32[8192]{0:T(1024)S(1)}, f32[8192,2048]{0,1:T(8,128)}) fusion(f32[2048]{0:T(1024)} %param.10, bf16[8192,384]{1,0:T(8,128)(2,1)} %all-gather.3.cloned.1.call-done, bf16[2048,384]{1,0:T(8,128)(2,1)S(1)} %copy-done), kind=kOutput, calls=%fused_computation.7 | convolution fusion | flops 12918448128 | bytes 75014144 | tf_op jit(solution)/shard_map/dot_general | solution.py:17
  88.5 44.5 %pmax.7 = f32[8192]{0:T(1024)S(1)} all-reduce(f32[8192]{0:T(1024)S(1)} %get-tuple-element.20), channel_id=1, replica_groups=mesh['dp'=1,'tp'=32] {'tp'}, use_global_device_ids=true, to_apply=%region_1.2 | all-reduce | flops 8192 | bytes 65536 | tf_op jit(solution)/shard_map/pmax | solution.py:24
  133.0 25.2 %fusion.2 = (f32[8192]{0:T(1024)S(1)}, f32[8192]{0:T(1024)S(1)}) fusion(f32[8192,2048]{0,1:T(8,128)} %get-tuple-element.21, f32[8192]{0:T(1024)S(1)} %get-tuple-element.20, f32[2048]{0:T(1024)S(1)} %copy-done.3, s32[8192]{0:T(1024)S(1)} %bitcast.22), kind=kLoop, calls=%fused_computation.6 | loop fusion | flops 100646912 | bytes 67248128 | tf_op jit(solution)/shard_map/reduce_sum | solution.py:23
  158.3 0.7 pad_maximum_fusion
  159.0 0.1 all-reduce.4.cloned.1.call-update
  159.0 0.2 reduce-scatter.2.cloned.1.call-start
  159.3 88.6 %all-reduce.4.cloned.1.call-done = f32[2,8192]{1,0:T(2,128)} async-done(((f32[2,8192]{1,0:T(2,128)}), f32[2,8192]{1,0:T(2,128)}) %all-reduce.4.cloned.1.call-update) | async-done | bytes 65552 | tf_op jit(solution)/shard_map/psum | solution.py:26
  247.9 1.0 fusion.14
  248.9 0.6 fusion.9
  249.5 33.7 %fusion.1 = bf16[8192,2048]{0,1:T(8,128)(2,1)} fusion(f32[8192,2048]{0,1:T(8,128)} %get-tuple-element.21, f32[8192]{0:T(1024)S(1)} %get-tuple-element.16, s32[8192]{0:T(1024)S(1)} %bitcast.23, f32[8192]{0:T(1024)S(1)} %get-tuple-element.20, f32[2048]{0:T(1024)S(1)} %copy-done.3), kind=kLoop, calls=%fused_computation.2 | loop fusion | flops 134217728 | bytes 100769792 | tf_op jit(solution)/shard_map/convert_element_type | solution.py:30
  283.2 24.8 %fusion.16 = f32[8192,384]{1,0:T(8,128)} fusion(bf16[8192,2048]{0,1:T(8,128)(2,1)} %fusion.1, bf16[2048,384]{1,0:T(8,128)(2,1)S(1)} %copy-done), kind=kOutput, calls=%fused_computation.29 | convolution fusion | flops 12884901888 | bytes 47710208 | tf_op jit(solution)/shard_map/dot_general | solution.py:32
  308.7 23.9 %convolution_convert_fusion = bf16[2048,384]{1,0:T(8,128)(2,1)} fusion(bf16[8192,2048]{0,1:T(8,128)(2,1)} %fusion.1, bf16[8192,384]{1,0:T(8,128)(2,1)} %all-gather.3.cloned.1.call-done), kind=kOutput, calls=%fused_computation.10 | convolution fusion | flops 12885688320 | bytes 41418752 | tf_op jit(solution)/shard_map/dot_general | solution.py:31
  332.6 70.1 %reduce-scatter.2.cloned.1.call-done = f32[256,384]{1,0:T(8,128)} async-done(((f32[8192,384]{1,0:T(8,128)}), f32[256,384]{1,0:T(8,128)}) %reduce-scatter.2.cloned.1.call-update) | async-done | bytes 393232 | tf_op jit(solution)/shard_map/reduce_scatter | solution.py:33
  402.7 3.1 fusion.5
  405.8 3.8 convolution_bitcast_fusion
  409.6 81.2 %all-reduce.5 = (bf16[384,1536]{0,1:T(8,128)(2,1)S(1)}, bf16[1536,384]{1,0:T(8,128)(2,1)}) all-reduce(f32[384,1536]{0,1:T(8,128)} %convolution_bitcast_fusion, f32[1536,384]{1,0:T(8,128)} %fusion.5), channel_id=1, replica_groups=mesh['dp'=1,'tp'=32] {'tp'}, use_global_device_ids=true, to_apply=%region_7.8 | all-reduce | flops 1179648 | bytes 7077888 | tf_op jit(solution)/shard_map/psum | solution.py:38
  490.8 1.4 copy.11
  (11 shorter events, 0.1 us)
Async XLA Ops:
  7.2 53.0 %copy-start = (bf16[2048,384]{1,0:T(8,128)(2,1)S(1)}, bf16[2048,384]{1,0:T(8,128)(2,1)}, u32[]{:S(2)}) copy-start(bf16[2048,384]{1,0:T(8,128)(2,1)} %param.9) | copy-start | bytes 4718596
  7.2 53.0 %all-gather.3.cloned.1.call-start = ((), (), s32[]{:S(2)}) async-start(), calls=%async_computation.1 | async-start | bytes 6488064 | tf_op jit(solution)/shard_map/all_gather | solution.py:14
  11.9 236.0 %all-reduce.4.cloned.1.call-start = ((), (), s32[]{:S(2)}) async-start(), calls=%async_computation.2 | async-start | bytes 131072 | tf_op jit(solution)/shard_map/psum | solution.py:26
  43.7 89.3 %copy-start.3 = (f32[2048]{0:T(1024)S(1)}, f32[2048]{0:T(1024)}, u32[]{:S(2)}) copy-start(f32[2048]{0:T(1024)} %param.10) | copy-start | bytes 24580
  159.0 243.7 %reduce-scatter.2.cloned.1.call-start = ((), (), s32[]{:S(2)}) async-start(), calls=%async_computation.3 | async-start | bytes 12976128 | tf_op jit(solution)/shard_map/reduce_scatter | solution.py:33
  308.7 97.1 %copy-start.2 = (bf16[256,384]{1,0:T(8,128)(2,1)S(1)}, bf16[256,384]{1,0:T(8,128)(2,1)}, u32[]{:S(2)}) copy-start(bf16[256,384]{1,0:T(8,128)(2,1)} %param.6) | copy-start | bytes 589828
  402.7 89.5 %copy-start.1 = (bf16[2048,384]{1,0:T(8,128)(2,1)S(1)}, bf16[2048,384]{1,0:T(8,128)(2,1)}, u32[]{:S(2)}) copy-start(bf16[2048,384]{1,0:T(8,128)(2,1)} %param.9) | copy-start | bytes 4718596
Sparse Core Ops, SparseCore 0:
  12.0 48.0 all-gather.2
  159.1 88.7 all-reduce.3
  308.1 94.4 reduce-scatter.1
where the time goes:
time: 501 us; the launch traced here: 500 us
  waiting for transfers between devices  175 us (35%)
  blocking collectives  157 us (31%)
  matrix products  88.6 us (18%)
  other arithmetic  60.2 us (12%)
  between operations  15.6 us (3%)
    psum x1, waiting for transfers between devices, local_step(): row_stats = lax.psum(jnp.stack([local_sum * rescale, local_target]), 'tp')  88.6 us
    psum x1, blocking collectives, local_step(): grad_first, grad_second = lax.psum((first_part, second_part), 'tp')  81.2 us
    reduce_scatter x1, waiting for transfers between devices, local_step(): lax.psum_scatter(emb_part, 'tp', scatter_dimension=0, tiled=True)  70.1 us
    pmax x1, blocking collectives, local_step(): row_max = lax.pmax(local_max, 'tp')  44.5 us
    convert_element_type x1, other arithmetic, local_step(): (jnp.where(label_hit, soft_prob - 1.0, soft_prob) / total_rows).astype(jn...  33.7 us
    all_gather x1, blocking collectives, local_step(): labels_all = lax.all_gather(labels, 'tp', axis=0, tiled=True)  31.7 us
    dot_general x1, matrix products, local_step(): lax.dot_general(emb_all, catalogue, (((1,), (1,)), ((), ())), preferred_e...  28.3 us
    reduce_sum x1, other arithmetic, local_step(): local_sum = jnp.sum(exp_local, axis=1)  25.2 us
  transfers between devices with their start and end apart: 3, of which 3 were waited for; matrix products, arithmetic and copies ran while one was open for 5% of the time, Pallas kernels for 0%

commit v1 on v0

v1 whole, which is shorter than its diff:
```python
import functools
import math

import jax
import jax.numpy as jnp
from jax import lax
from jax.experimental import pallas as pl
from jax.experimental.pallas import tpu as pltpu
from jax.sharding import PartitionSpec as P

MESH = pl.DeviceIdType.MESH
SIDE = 4
ORDER = ((0, 0), (1, 0), (3, 0), (2, 0), (0, 1), (0, 3), (1, 1), (1, 3), (3, 1), (3, 3), (2, 1), (2, 3), (0, 2), (1, 2), (3, 2), (2, 2))
POS = {slot: k for k, slot in enumerate(ORDER)}
MESSAGES = [((0, 0), (1, 0), None, 0, -1), ((0, 0), (3, 0), None, 0, 1), ((1, 0), (2, 0), 0, 0, -1), ((3, 0), (2, 0), 1, 0, 1)]
for _u in range(SIDE):
    MESSAGES += [((_u, 0), (_u, 1), None, 1, -1), ((_u, 0), (_u, 3), None, 1, 1), ((_u, 1), (_u, 2), 0, 1, -1), ((_u, 3), (_u, 2), 1, 1, 1)]
NMSG = len(MESSAGES)
FULL = [i for i, msg in enumerate(MESSAGES) if msg[2] is None]
PART = [i for i, msg in enumerate(MESSAGES) if msg[2] is not None]
BF16, F32 = jnp.bfloat16, jnp.float32


def nt(a, b):
    return lax.dot_general(a, b, (((1,), (1,)), ((), ())), preferred_element_type=F32)


def nn(a, b):
    return jnp.dot(a, b, preferred_element_type=F32)


def kernel(
    cfg, q_ref, w1_ref, w2_ref, lab_ref, e_hbm, lq_hbm, de_out, dw_out, loss_out,
    xg, eall, ets, lqs, act, hid, de, der, part_x, rbf, rbp, sto, sti, bco, bci, dw, dwr, pb, rwf, rwp, gb, ls, lp, lsum, lb,
    loc_sem, d2d_s, d2d_r, ag_s, ag_r, st_s, st_r, bc_s, bc_r, rs_s, rs_r, rw_s, rw_r, gw_s, gw_r, lb_s, lb_r,
):
    n, total_rows, tile = cfg
    chips = n // 2
    me = lax.axis_index("tp")
    core = lax.rem(me, 2)
    chip = me // 2
    cx, cy = lax.rem(chip, SIDE), chip // SIDE
    other = 1 - core
    rows, dim = q_ref.shape
    half = rows // 2
    items = e_hbm.shape[0]
    pair_items = 2 * items
    ntile = pair_items // tile

    def chip_at(dx, dy):
        return lax.rem(cy + (dy % SIDE), SIDE) * SIDE + lax.rem(cx + (dx % SIDE), SIDE)

    def dev(dx, dy):
        return chip_at(dx, dy) * 2 + core

    partner = chip * 2 + other

    def along(h, axis, step):
        return dev(step, 0) if axis == h else dev(0, step)

    def owner_off(h, slot):
        return slot if h == 0 else (slot[1], slot[0])

    def remote(src, dst, ssem, rsem, device):
        return pltpu.make_async_remote_copy(src_ref=src, dst_ref=dst, send_sem=ssem, recv_sem=rsem, device_id={"tp": device}, device_id_type=MESH)

    peers = [(dx, dy) for dy in range(SIDE) for dx in range(SIDE) if (dx, dy) != (0, 0)]
    barrier = pltpu.get_barrier_semaphore()
    for dx, dy in peers:
        pl.semaphore_signal(barrier, inc=1, device_id={"tp": dev(dx, dy)}, device_id_type=MESH)
    pl.semaphore_signal(barrier, inc=1, device_id={"tp": partner}, device_id_type=MESH)

    base = pl.multiple_of(core * items, items)
    mine = pl.ds(base, items)
    load_e = pltpu.make_async_copy(e_hbm, eall.at[mine], loc_sem.at[0])
    load_l = pltpu.make_async_copy(lq_hbm, lqs.at[mine], loc_sem.at[1])
    load_e.start()
    load_l.start()

    sto[...] = jnp.zeros_like(sto)
    bco[...] = jnp.zeros_like(bco)

    pre = nn(q_ref[...], w1_ref[...])
    act[...] = pre
    hid[...] = jnp.maximum(pre, 0.0).astype(BF16)
    emb = nn(hid[...], w2_ref[...]).astype(BF16)
    xg[0] = emb.reshape(2, half, dim)

    pl.semaphore_wait(barrier, len(peers) + 1)
    send_e = remote(e_hbm, eall.at[mine], d2d_s.at[0], d2d_r.at[0], partner)
    send_l = remote(lq_hbm, lqs.at[mine], d2d_s.at[1], d2d_r.at[1], partner)
    send_e.start()
    send_l.start()

    def tree(loc, ssem, rsem):
        def copy(i, h):
            src, dst, part, axis, step = MESSAGES[i]
            return remote(loc(src, h, part), loc(dst, h, part), ssem.at[i, h], rsem.at[i, h], along(h, axis, step))

        def arrived(slot):
            for i, msg in enumerate(MESSAGES):
                if msg[1] == slot:
                    for h in range(2):
                        copy(i, h).wait_recv()

        def forward(slot):
            for i, msg in enumerate(MESSAGES):
                if msg[0] == slot:
                    for h in range(2):
                        copy(i, h).start()

        def drain():
            for i in range(NMSG):
                for h in range(2):
                    copy(i, h).wait_send()

        return arrived, forward, drain

    def reverse_tree(acc, box, add, ssem, rsem):
        def copy(i, h):
            src, dst, part, axis, step = MESSAGES[i]
            return remote(acc(dst, h, part), box(i, h), ssem.at[i, h], rsem.at[i, h], along(h, axis, -step))

        def settle(slot):
            for i, msg in enumerate(MESSAGES):
                if msg[0] == slot:
                    for h in range(2):
                        copy(i, h).wait_recv()
                        add(i, h)
            for i, msg in enumerate(MESSAGES):
                if msg[1] == slot:
                    for h in range(2):
                        copy(i, h).start()

        def drain():
            for i in range(NMSG):
                for h in range(2):
                    copy(i, h).wait_send()

        return settle, drain

    quarter = half // 2

    def loc_x(slot, h, part):
        k = POS[slot]
        return xg.at[k, h] if part is None else xg.at[k, h, pl.ds(part * quarter, quarter)]

    x_arrived, x_forward, x_drain = tree(loc_x, ag_s, ag_r)
    x_forward((0, 0))

    load_e.wait()
    load_l.wait()
    send_e.wait_recv()
    send_l.wait_recv()

    @pl.loop(0, ntile)
    def _(i):
        ets[i] = eall[pl.ds(pl.multiple_of(i * tile, tile), tile), :].T

    @pl.loop(0, len(ORDER))
    def _(t):
        for k in range(1, len(ORDER)):
            @pl.when(t == k)
            def _(k=k):
                x_arrived(ORDER[k])
                x_forward(ORDER[k])

        xk = xg[t].reshape(rows, dim)

        def one(i, carry):
            m, s = carry
            at = pl.ds(pl.multiple_of(i * tile, tile), tile)
            lq = lqs[at, :]
            z = nt(eall[at, :], xk) - jnp.concatenate([lq, lq], axis=1)
            z = z.reshape(tile // 8, 8, rows)
            top = jnp.maximum(m, jnp.max(z, axis=0))
            s = s * jnp.exp(m - top) + jnp.sum(jnp.exp(z - top[None]), axis=0)
            return top, s

        m, s = lax.fori_loop(0, ntile, one, (jnp.full((8, rows), -jnp.inf, F32), jnp.zeros((8, rows), F32)))
        top = jnp.max(m, axis=0, keepdims=True)
        s = jnp.sum(s * jnp.exp(m - top), axis=0, keepdims=True)
        for h in range(2):
            lanes = slice(h * half, (h + 1) * half)
            sto[t, h, 0:1, :] = top[:, lanes]
            sto[t, h, 1:2, :] = s[:, lanes]

    def back(slot):
        return ((-slot[0]) % SIDE, (-slot[1]) % SIDE)

    def stat_copy(k, h):
        return remote(sto.at[k, h], sti.at[POS[back(ORDER[k])], h], st_s.at[k, h], st_r.at[POS[back(ORDER[k])], h], dev(*owner_off(h, ORDER[k])))

    def stat_recv(k, h):
        return remote(sto.at[k, h], sti.at[k, h], st_s.at[k, h], st_r.at[k, h], me)

    for k in range(1, chips):
        for h in range(2):
            stat_copy(k, h).start()
    for h in range(2):
        sti[0, h] = sto[0, h]
    for k in range(1, chips):
        for h in range(2):
            stat_recv(k, h).wait_recv()
    for h in range(2):
        tops = [sti[k, h, 0:1, :] for k in range(chips)]
        sums = [sti[k, h, 1:2, :] for k in range(chips)]
        top = functools.reduce(jnp.maximum, tops)
        s = functools.reduce(jnp.add, [sm * jnp.exp(tp - top) for tp, sm in zip(tops, sums)])
        bco[h, 0:1, :] = top + jnp.log(s) + math.log(total_rows)
        bco[h, 1:2, :] = lab_ref[0:1, h * half:(h + 1) * half]
        bci[0, h] = bco[h]

    def bc_copy(k, h):
        return remote(bco.at[h], bci.at[POS[back(ORDER[k])], h], bc_s.at[k, h], bc_r.at[POS[back(ORDER[k])], h], dev(*owner_off(h, ORDER[k])))

    def bc_recv(k, h):
        return remote(bco.at[h], bci.at[k, h], bc_s.at[k, h], bc_r.at[k, h], me)

    for k in range(1, chips):
        for h in range(2):
            bc_copy(k, h).start()

    lsum[...] = jnp.zeros_like(lsum)
    de[...] = jnp.zeros_like(de)
    for k in range(1, chips):
        for h in range(2):
            bc_recv(k, h).wait_recv()

    lo_x = dim // 2

    def acc_x(slot, h, part):
        k = POS[slot]
        return part_x.at[k, h] if part is None else part_x.at[k, h, pl.ds(part * lo_x, lo_x)]

    def box_x(i, h):
        return rbf.at[FULL.index(i), h] if i in FULL else rbp.at[PART.index(i), h]

    def add_x(i, h):
        ref = acc_x(MESSAGES[i][0], h, MESSAGES[i][2])
        ref[...] = ref[...] + box_x(i, h)[...]

    x_settle, px_drain = reverse_tree(acc_x, box_x, add_x, rs_s, rs_r)
    first_item = chip * pair_items

    @pl.loop(0, len(ORDER))
    def _(s):
        t = len(ORDER) - 1 - s
        xk = xg[t].reshape(rows, dim)
        lse = jnp.concatenate([bci[t, 0, 0:1, :], bci[t, 1, 0:1, :]], axis=1)
        lab = jnp.concatenate([bci[t, 0, 1:2, :], bci[t, 1, 1:2, :]], axis=1).astype(jnp.int32) - first_item

        @pl.loop(0, ntile)
        def _(i):
            at = pl.ds(pl.multiple_of(i * tile, tile), tile)
            lq = lqs[at, :]
            z = nt(eall[at, :], xk) - jnp.concatenate([lq, lq], axis=1) - lse
            hit = lax.broadcasted_iota(jnp.int32, (tile, rows), 0) == lab - i * tile
            g = (jnp.exp(z) - jnp.where(hit, 1.0 / total_rows, 0.0)).astype(BF16)
            lsum[...] += jnp.sum(jnp.where(hit, z, 0.0).reshape(tile // 8, 8, rows), axis=0)
            de[at, :] += nn(g, xk)
            dx = nn(ets[i], g)

            @pl.when(i == 0)
            def _():
                for h in range(2):
                    part_x[t, h] = dx[:, h * half:(h + 1) * half]

            @pl.when(i > 0)
            def _():
                for h in range(2):
                    part_x[t, h] += dx[:, h * half:(h + 1) * half]

        for k in range(len(ORDER)):
            @pl.when(t == k)
            def _(k=k):
                x_settle(ORDER[k])

    theirs = pl.ds(pl.multiple_of(other * items, items), items)
    send_de = remote(de.at[theirs], der, d2d_s.at[2], d2d_r.at[2], partner)
    send_de.start()
    ls[...] = lsum[:, :half] + lsum[:, half:]
    send_ls = remote(ls, lp, d2d_s.at[3], d2d_r.at[3], partner)
    send_ls.start()

    dxt = jnp.concatenate([part_x[0, 0], part_x[0, 1]], axis=1)
    dx = dxt.T.astype(BF16)
    dw[1] = nn(dxt.astype(BF16), hid[...])
    dh = nt(dx, w2_ref[...])
    da = jnp.where(act[...] > 0.0, dh, 0.0).astype(BF16)
    dw[0] = nn(q_ref[...].T, da)
    send_dw = remote(dw.at[other], dwr, d2d_s.at[4], d2d_r.at[4], partner)
    send_dw.start()

    send_ls.wait()
    ls2 = lb.at[chip]
    lsum[:, :half] = ls[...] + lp[...]
    lsum_src = lsum.at[:, pl.ds(0, half)]
    ls2[...] = lsum[:, :half]

    def lb_copy(k):
        return remote(lsum_src, lb.at[chip], lb_s.at[k], lb_r.at[POS[back(ORDER[k])]], dev(*ORDER[k]))

    def lb_recv(k):
        return remote(lsum_src, lb.at[chip_at(*ORDER[k])], lb_s.at[k], lb_r.at[k], me)

    for k in range(1, chips):
        lb_copy(k).start()

    block = dim // (2 * SIDE)
    width = w1_ref.shape[1] // SIDE

    def where_w(k, h):
        ox, oy = owner_off(h, ORDER[k])
        r = (lax.rem(cy + oy, SIDE) * 2 + h) * block
        c = lax.rem(cx + ox, SIDE) * width
        return pl.ds(pl.multiple_of(r, block), block), pl.ds(pl.multiple_of(c, width), width)

    send_dw.wait()
    for k in range(chips):
        for h in range(2):
            r, c = where_w(k, h)
            pb[k, h] = dw[core, r, c] + dwr[r, c]

    lo_w = block // 2

    def acc_w(slot, h, part):
        k = POS[slot]
        return pb.at[k, h] if part is None else pb.at[k, h, pl.ds(part * lo_w, lo_w)]

    def box_w(i, h):
        return rwf.at[FULL.index(i), h] if i in FULL else rwp.at[PART.index(i), h]

    def add_w(i, h):
        ref = acc_w(MESSAGES[i][0], h, MESSAGES[i][2])
        ref[...] = ref[...] + box_w(i, h)[...]

    w_settle, pw_drain = reverse_tree(acc_w, box_w, add_w, rw_s, rw_r)
    for slot in reversed(ORDER):
        w_settle(slot)

    gb[core, 0] = pb[0].astype(BF16)
    cuts = (pl.ds(0, 32), pl.ds(32, block - 32))

    def loc_g(slot, h, part):
        k = POS[slot]
        return gb.at[core, k, h] if part is None else gb.at[core, k, h, cuts[part]]

    g_arrived, g_forward, g_drain = tree(loc_g, gw_s, gw_r)
    g_forward((0, 0))

    send_de.wait()
    de_out[...] = (de[mine, :] + der[...]).astype(BF16)
    for k in range(1, chips):
        lb_recv(k).wait_recv()
    tot = functools.reduce(jnp.add, [lb[k] for k in range(chips)])
    mean = -jnp.sum(tot, keepdims=True) / total_rows - math.log(total_rows)
    loss_out[...] = jnp.broadcast_to(mean, loss_out.shape)

    for slot in ORDER[1:]:
        g_arrived(slot)
        g_forward(slot)
    send_gb = remote(gb.at[core], gb.at[core], d2d_s.at[5], d2d_r.at[5], partner)
    send_gb.start()
    send_gb.wait()
    for o in range(2):
        for k in range(chips):
            for h in range(2):
                r, c = where_w(k, h)
                dw_out[o, r, c] = gb[o, k, h]

    send_e.wait_send()
    send_l.wait_send()
    x_drain()
    px_drain()
    pw_drain()
    g_drain()
    for k in range(1, chips):
        lb_copy(k).wait_send()
        for h in range(2):
            stat_copy(k, h).wait_send()
            bc_copy(k, h).wait_send()


def solution(mesh):
    n = mesh.shape["tp"]

    def local_step(queries, w_first, w_second, catalogue, log_q, labels):
        rows, dim = queries.shape
        hidden = w_first.shape[1]
        items = catalogue.shape[0]
        total_rows = rows * n
        tile = 512
        half = rows // 2
        chips = n // 2
        lab = jnp.broadcast_to(labels.astype(F32)[None, :], (8, rows))
        lq = jnp.broadcast_to(log_q[:, None], (items, 128))
        dma = pltpu.SemaphoreType.DMA
        vm = pltpu.VMEM
        block, width = dim // (2 * SIDE), hidden // SIDE
        vspec = pl.BlockSpec(memory_space=pltpu.VMEM)
        aspec = pl.BlockSpec(memory_space=pl.ANY)
        de, dw, loss = pl.pallas_call(
            functools.partial(kernel, (n, total_rows, tile)),
            out_shape=[
                jax.ShapeDtypeStruct((items, dim), BF16),
                jax.ShapeDtypeStruct((2, dim, hidden), BF16),
                jax.ShapeDtypeStruct((8, 128), F32),
            ],
            in_specs=[vspec] * 4 + [aspec] * 2,
            out_specs=[vspec] * 3,
            scratch_shapes=[
                vm((chips, 2, half, dim), BF16),
                vm((2 * items, dim), BF16),
                vm((2 * items // tile, dim, tile), BF16),
                vm((2 * items, 128), F32),
                vm((rows, hidden), F32),
                vm((rows, hidden), BF16),
                vm((2 * items, dim), F32),
                vm((items, dim), F32),
                vm((chips, 2, dim, half), F32),
                vm((len(FULL), 2, dim, half), F32),
                vm((len(PART), 2, dim // 2, half), F32),
                vm((chips, 2, 8, half), F32),
                vm((chips, 2, 8, half), F32),
                vm((2, 8, half), F32),
                vm((chips, 2, 8, half), F32),
                vm((2, dim, hidden), F32),
                vm((dim, hidden), F32),
                vm((chips, 2, block, width), F32),
                vm((len(FULL), 2, block, width), F32),
                vm((len(PART), 2, block // 2, width), F32),
                vm((2, chips, 2, block, width), BF16),
                vm((8, half), F32),
                vm((8, half), F32),
                vm((8, rows), F32),
                vm((chips, 8, half), F32),
                dma((2,)), dma((6,)), dma((6,)),
                dma((NMSG, 2)), dma((NMSG, 2)),
                dma((chips, 2)), dma((chips, 2)),
                dma((chips, 2)), dma((chips, 2)),
                dma((NMSG, 2)), dma((NMSG, 2)),
                dma((NMSG, 2)), dma((NMSG, 2)),
                dma((NMSG, 2)), dma((NMSG, 2)),
                dma((chips,)), dma((chips,)),
            ],
            compiler_params=pltpu.CompilerParams(collective_id=0, has_side_effects=True, vmem_limit_bytes=67_043_328),
        )(queries, w_first, w_second, lab, catalogue, lq)
        return loss[0, :1], de, dw[0], dw[1].T

    row_spec = P(("dp", "tp"), None)
    return jax.shard_map(
        local_step,
        mesh=mesh,
        in_specs=(row_spec, P(None, None), P(None, None), P("tp", None), P("tp"), P(("dp", "tp"))),
        out_specs=(P("dp"), row_spec, P("dp", None), P("dp", None)),
        check_vma=False,
    )
```

time: 501 us -> 275 us (0.55)
  Pallas kernels: 0 us -> 264 us
  waiting for transfers between devices: 175 us -> 0 us
  blocking collectives: 157 us -> 0 us
  matrix products: 88.6 us -> 0 us
  other arithmetic: 60.2 us -> 0.68 us
  between operations: 15.6 us -> 0.64 us
  local copies, waits for them, and re-layouts: 2.44 us -> 9.43 us
    pallas_call x0 -> x1, Pallas kernels: none -> 264 us  [local_step(): pl.pallas_call(functools.partial(kernel, (n, total_rows, tile)), out_shap...]
    psum x1 -> x0, waiting for transfers between devices: 88.6 us -> none  [local_step(): row_stats = lax.psum(jnp.stack([local_sum * rescale, local_target]), 'tp')]
    dot_general x7 -> x0, matrix products: 88.6 us -> none  [the longest x1 28.3 us: local_step(): lax.dot_general(emb_all, catalogue, (((1,), (1,)), ((), ())), preferred_e...]
    psum x1 -> x0, blocking collectives: 81.2 us -> none  [local_step(): grad_first, grad_second = lax.psum((first_part, second_part), 'tp')]
    reduce_scatter x1 -> x0, waiting for transfers between devices: 70.1 us -> none  [local_step(): lax.psum_scatter(emb_part, 'tp', scatter_dimension=0, tiled=True)]
    pmax x1 -> x0, blocking collectives: 44.5 us -> none  [local_step(): row_max = lax.pmax(local_max, 'tp')]
    convert_element_type x1, other arithmetic: 33.7 us -> 0.68 us  [local_step(): lab = jnp.broadcast_to(labels.astype(F32)[None, :], (8, rows))]
    all_gather x1 -> x0, blocking collectives: 31.7 us -> none  [local_step(): labels_all = lax.all_gather(labels, 'tp', axis=0, tiled=True)]
  transfers between devices with their start and end apart: 3 -> 0, of which waited for: 3 -> 0; matrix products, arithmetic and copies ran while one was open for 5% -> 0% of each run, Pallas kernels for 0% -> 0%
where the time goes in v1:
time: 275 us
  Pallas kernels  264 us (96%)
  local copies, waits for them, and re-layouts  9.43 us (3%)
    pallas_call x1, Pallas kernels, local_step(): pl.pallas_call(functools.partial(kernel, (n, total_rows, tile)), out_shap...  264 us

profile of v1, /device:TPU:97, one launch (start us, length us, event | category | flops | bytes accessed | tf_op | source)
XLA Modules:
  0.0 274.5 jit_solution(17805245169161789271)
XLA Ops:
  0.6 0.7 convert_element_type.3
  1.3 0.6 broadcast_in_dim.4.lab_ref
  1.9 2.0 broadcast_in_dim.5.lq_hbm
  3.9 263.8 %shard_map.93 = (bf16[2048,384]{1,0:T(8,128)(2,1)}, bf16[2,384,1536]{2,1,0:T(8,128)(2,1)}, f32[8,128]{1,0:T(8,128)}) custom-call(bf16[256,384]{1,0:T(8,128)(2,1)} %q_ref.1, bf16[384,1536]{1,0:T(8,128)(2,1)} %w1_ref.1, bf16[1536,384]{1,0:T(8,128)(2,1)} %w2_ref.1, f32[8,256]{1,0:T(8,128)} %broadcast_in_dim.4.lab_ref, bf16[2048,384]{1,0:T(8,128)(2,1)} %e_hbm.1, ...), custom_call_target="tpu_custom_call" | custom-call | tf_op jit(solution)/shard_map/pallas_call | solution.py:403
  267.7 1.2 slice.9
  268.9 2.8 %slice_bitcast_fusion = (bf16[1536,384]{0,1:T(8,128)(2,1)S(1)}, bf16[384,1536]{1,0:T(8,128)(2,1)}) fusion(bf16[2,384,1536]{2,1,0:T(8,128)(2,1)} %get-tuple-element.9), kind=kLoop, calls=%fused_computation | loop fusion | bytes 4718592 | tf_op jit(solution)/shard_map/transpose | solution.py:449
  271.7 0.0 copy-start
  271.7 1.4 copy.10
  273.1 0.3 copy-done
  273.4 1.1 copy.12
Async XLA Ops:
  271.7 1.7 copy-start

commit v2 on v1

--- a/solution.py
+++ b/solution.py
@@ -31,7 +31,7 @@
 
 def kernel(
     cfg, q_ref, w1_ref, w2_ref, lab_ref, e_hbm, lq_hbm, de_out, dw_out, loss_out,
-    xg, eall, ets, lqs, act, hid, de, der, part_x, rbf, rbp, sto, sti, bco, bci, dw, dwr, pb, rwf, rwp, gb, ls, lp, lsum, lb,
+    xg, eall, ets, lqs, act, hid, de, der, part_x, rbf, rbp, sto, sti, bco, bci, dw, dwr, pb, rwf, rwp, gb, ls, lp, lsum, lb, lqc, za, zb, ga, gbt,
     loc_sem, d2d_s, d2d_r, ag_s, ag_r, st_s, st_r, bc_s, bc_r, rs_s, rs_r, rw_s, rw_r, gw_s, gw_r, lb_s, lb_r,
 ):
     n, total_rows, tile = cfg
@@ -73,24 +73,24 @@
     base = pl.multiple_of(core * items, items)
     mine = pl.ds(base, items)
     load_e = pltpu.make_async_copy(e_hbm, eall.at[mine], loc_sem.at[0])
-    load_l = pltpu.make_async_copy(lq_hbm, lqs.at[mine], loc_sem.at[1])
+    load_l = pltpu.make_async_copy(lq_hbm, lqc.at[core], loc_sem.at[1])
     load_e.start()
     load_l.start()
 
     sto[...] = jnp.zeros_like(sto)
     bco[...] = jnp.zeros_like(bco)
+
+    pl.semaphore_wait(barrier, len(peers) + 1)
+    send_e = remote(e_hbm, eall.at[mine], d2d_s.at[0], d2d_r.at[0], partner)
+    send_l = remote(lq_hbm, lqc.at[core], d2d_s.at[1], d2d_r.at[1], partner)
+    send_l.start()
+    send_e.start()
 
     pre = nn(q_ref[...], w1_ref[...])
     act[...] = pre
     hid[...] = jnp.maximum(pre, 0.0).astype(BF16)
     emb = nn(hid[...], w2_ref[...]).astype(BF16)
     xg[0] = emb.reshape(2, half, dim)
-
-    pl.semaphore_wait(barrier, len(peers) + 1)
-    send_e = remote(e_hbm, eall.at[mine], d2d_s.at[0], d2d_r.at[0], partner)
-    send_l = remote(lq_hbm, lqs.at[mine], d2d_s.at[1], d2d_r.at[1], partner)
-    send_e.start()
-    send_l.start()
 
     def tree(loc, ssem, rsem):
         def copy(i, h):
@@ -148,36 +148,58 @@
     x_arrived, x_forward, x_drain = tree(loc_x, ag_s, ag_r)
     x_forward((0, 0))
 
+    load_l.wait()
+    send_l.wait_recv()
+
+    @pl.loop(0, 2)
+    def _(o):
+        @pl.loop(0, items // 128)
+        def _(j):
+            row = lqc[o, pl.ds(j, 1), :]
+            lqs[pl.ds(pl.multiple_of(o * items + j * 128, 128), 128), :] = jnp.broadcast_to(row, (128, 128)).T
+
     load_e.wait()
-    load_l.wait()
     send_e.wait_recv()
-    send_l.wait_recv()
 
     @pl.loop(0, ntile)
     def _(i):
         ets[i] = eall[pl.ds(pl.multiple_of(i * tile, tile), tile), :].T
 
-    @pl.loop(0, len(ORDER))
+    nslot = len(ORDER)
+
+    def rows_of(i):
+        return pl.ds(pl.multiple_of(i * tile, tile), tile)
+
+    def logits(t, i):
+        lq = lqs[rows_of(i), :]
+        return nt(eall[rows_of(i), :], xg[t].reshape(rows, dim)) - jnp.concatenate([lq, lq], axis=1)
+
+    def online(z_ref, carry):
+        m, s = carry
+        z = z_ref[...].reshape(tile // 8, 8, rows)
+        top = jnp.maximum(m, jnp.max(z, axis=0))
+        return top, s * jnp.exp(m - top) + jnp.sum(jnp.exp(z - top[None]), axis=0)
+
+    za[...] = logits(0, 0)
+
+    @pl.loop(0, nslot)
     def _(t):
-        for k in range(1, len(ORDER)):
-            @pl.when(t == k)
-            def _(k=k):
-                x_arrived(ORDER[k])
-                x_forward(ORDER[k])
-
-        xk = xg[t].reshape(rows, dim)
-
-        def one(i, carry):
-            m, s = carry
-            at = pl.ds(pl.multiple_of(i * tile, tile), tile)
-            lq = lqs[at, :]
-            z = nt(eall[at, :], xk) - jnp.concatenate([lq, lq], axis=1)
-            z = z.reshape(tile // 8, 8, rows)
-            top = jnp.maximum(m, jnp.max(z, axis=0))
-            s = s * jnp.exp(m - top) + jnp.sum(jnp.exp(z - top[None]), axis=0)
-            return top, s
-
-        m, s = lax.fori_loop(0, ntile, one, (jnp.full((8, rows), -jnp.inf, F32), jnp.zeros((8, rows), F32)))
+        def two(i, carry):
+            @pl.when(i == ntile // 2 - 1)
+            def _():
+                for k in range(1, nslot):
+                    @pl.when(t == k - 1)
+                    def _(k=k):
+                        x_arrived(ORDER[k])
+                        x_forward(ORDER[k])
+
+            last = (2 * i + 2) // ntile
+            zb[...] = logits(t, 2 * i + 1)
+            carry = online(za, carry)
+            za[...] = logits(jnp.minimum(t + last, nslot - 1), lax.rem(2 * i + 2, ntile))
+            return online(zb, carry)
+
+        m, s = lax.fori_loop(0, ntile // 2, two, (jnp.full((8, rows), -jnp.inf, F32), jnp.zeros((8, rows), F32)))
         top = jnp.max(m, axis=0, keepdims=True)
         s = jnp.sum(s * jnp.exp(m - top), axis=0, keepdims=True)
         for h in range(2):
@@ -199,6 +221,17 @@
             stat_copy(k, h).start()
     for h in range(2):
         sti[0, h] = sto[0, h]
+
+    @pl.loop(0, ntile)
+    def _(i):
+        de[rows_of(i), :] = jnp.zeros((tile, dim), F32)
+
+    @pl.loop(0, nslot)
+    def _(t):
+        part_x[t] = jnp.zeros((2, dim, half), F32)
+
+    lsum[...] = jnp.zeros_like(lsum)
+    gbt[...] = jnp.zeros_like(gbt)
     for k in range(1, chips):
         for h in range(2):
             stat_recv(k, h).wait_recv()
@@ -208,7 +241,7 @@
         top = functools.reduce(jnp.maximum, tops)
         s = functools.reduce(jnp.add, [sm * jnp.exp(tp - top) for tp, sm in zip(tops, sums)])
         bco[h, 0:1, :] = top + jnp.log(s) + math.log(total_rows)
-        bco[h, 1:2, :] = lab_ref[0:1, h * half:(h + 1) * half]
+        bco[h, 1:2, :] = lab_ref[0:1, h * half:(h + 1) * half].astype(F32)
         bci[0, h] = bco[h]
 
     def bc_copy(k, h):
@@ -221,8 +254,7 @@
         for h in range(2):
             bc_copy(k, h).start()
 
-    lsum[...] = jnp.zeros_like(lsum)
-    de[...] = jnp.zeros_like(de)
+    za[...] = logits(nslot - 1, 0)
     for k in range(1, chips):
         for h in range(2):
             bc_recv(k, h).wait_recv()
@@ -243,42 +275,48 @@
     x_settle, px_drain = reverse_tree(acc_x, box_x, add_x, rs_s, rs_r)
     first_item = chip * pair_items
 
-    @pl.loop(0, len(ORDER))
+    def soften(z_ref, g_ref, t, i):
+        lse = jnp.concatenate([bci[t, 0, 0:1, :], bci[t, 1, 0:1, :]], axis=1)
+        lab = jnp.concatenate([bci[t, 0, 1:2, :], bci[t, 1, 1:2, :]], axis=1).astype(jnp.int32) - (first_item + i * tile)
+        z = z_ref[...] - lse
+        hit = lax.broadcasted_iota(jnp.int32, (tile, rows), 0) == lab
+        g_ref[...] = (jnp.exp(z) - jnp.where(hit, 1.0 / total_rows, 0.0)).astype(BF16)
+        lsum[...] += jnp.sum(jnp.where(hit, z, 0.0).reshape(tile // 8, 8, rows), axis=0)
+
+    def spread(g_ref, t, i):
+        g = g_ref[...]
+        de[rows_of(i), :] += nn(g, xg[t].reshape(rows, dim))
+        dx = nn(ets[i], g)
+        for h in range(2):
+            part_x[t, h] += dx[:, h * half:(h + 1) * half]
+
+    @pl.loop(0, nslot)
     def _(s):
-        t = len(ORDER) - 1 - s
-        xk = xg[t].reshape(rows, dim)
-        lse = jnp.concatenate([bci[t, 0, 0:1, :], bci[t, 1, 0:1, :]], axis=1)
-        lab = jnp.concatenate([bci[t, 0, 1:2, :], bci[t, 1, 1:2, :]], axis=1).astype(jnp.int32) - first_item
-
-        @pl.loop(0, ntile)
+        t = nslot - 1 - s
+
+        @pl.loop(0, ntile // 2)
         def _(i):
-            at = pl.ds(pl.multiple_of(i * tile, tile), tile)
-            lq = lqs[at, :]
-            z = nt(eall[at, :], xk) - jnp.concatenate([lq, lq], axis=1) - lse
-            hit = lax.broadcasted_iota(jnp.int32, (tile, rows), 0) == lab - i * tile
-            g = (jnp.exp(z) - jnp.where(hit, 1.0 / total_rows, 0.0)).astype(BF16)
-            lsum[...] += jnp.sum(jnp.where(hit, z, 0.0).reshape(tile // 8, 8, rows), axis=0)
-            de[at, :] += nn(g, xk)
-            dx = nn(ets[i], g)
-
-            @pl.when(i == 0)
+            @pl.when(i == 1)
             def _():
-                for h in range(2):
-                    part_x[t, h] = dx[:, h * half:(h + 1) * half]
-
-            @pl.when(i > 0)
-            def _():
-                for h in range(2):
-                    part_x[t, h] += dx[:, h * half:(h + 1) * half]
-
-        for k in range(len(ORDER)):
-            @pl.when(t == k)
-            def _(k=k):
-                x_settle(ORDER[k])
+                for k in range(1, nslot):
+                    @pl.when(t + 1 == k)
+                    def _(k=k):
+                        x_settle(ORDER[k])
+
+            first = jnp.where(i == 0, 1, 0)
+            last = (2 * i + 2) // ntile
+            zb[...] = logits(t, 2 * i + 1)
+            soften(za, ga, t, 2 * i)
+            spread(gbt, jnp.minimum(t + first, nslot - 1), lax.rem(2 * i + ntile - 1, ntile))
+            za[...] = logits(jnp.maximum(t - last, 0), lax.rem(2 * i + 2, ntile))
+            soften(zb, gbt, t, 2 * i + 1)
+            spread(ga, t, 2 * i)
+
+    spread(gbt, 0, ntile - 1)
+    x_settle(ORDER[0])
 
     theirs = pl.ds(pl.multiple_of(other * items, items), items)
     send_de = remote(de.at[theirs], der, d2d_s.at[2], d2d_r.at[2], partner)
-    send_de.start()
     ls[...] = lsum[:, :half] + lsum[:, half:]
     send_ls = remote(ls, lp, d2d_s.at[3], d2d_r.at[3], partner)
     send_ls.start()
@@ -291,6 +329,7 @@
     dw[0] = nn(q_ref[...].T, da)
     send_dw = remote(dw.at[other], dwr, d2d_s.at[4], d2d_r.at[4], partner)
     send_dw.start()
+    send_de.start()
 
     send_ls.wait()
     ls2 = lb.at[chip]
@@ -354,8 +393,7 @@
     for k in range(1, chips):
         lb_recv(k).wait_recv()
     tot = functools.reduce(jnp.add, [lb[k] for k in range(chips)])
-    mean = -jnp.sum(tot, keepdims=True) / total_rows - math.log(total_rows)
-    loss_out[...] = jnp.broadcast_to(mean, loss_out.shape)
+    loss_out[0] = -jnp.sum(tot) / total_rows - math.log(total_rows)
 
     for slot in ORDER[1:]:
         g_arrived(slot)
@@ -393,8 +431,8 @@
         tile = 512
         half = rows // 2
         chips = n // 2
-        lab = jnp.broadcast_to(labels.astype(F32)[None, :], (8, rows))
-        lq = jnp.broadcast_to(log_q[:, None], (items, 128))
+        lab = labels.reshape(1, rows)
+        lq = log_q.reshape(items // 128, 128)
         dma = pltpu.SemaphoreType.DMA
         vm = pltpu.VMEM
         block, width = dim // (2 * SIDE), hidden // SIDE
@@ -405,10 +443,10 @@
             out_shape=[
                 jax.ShapeDtypeStruct((items, dim), BF16),
                 jax.ShapeDtypeStruct((2, dim, hidden), BF16),
-                jax.ShapeDtypeStruct((8, 128), F32),
+                jax.ShapeDtypeStruct((1,), F32),
             ],
             in_specs=[vspec] * 4 + [aspec] * 2,
-            out_specs=[vspec] * 3,
+            out_specs=[vspec] * 2 + [pl.BlockSpec(memory_space=pltpu.SMEM)],
             scratch_shapes=[
                 vm((chips, 2, half, dim), BF16),
                 vm((2 * items, dim), BF16),
@@ -435,6 +473,11 @@
                 vm((8, half), F32),
                 vm((8, rows), F32),
                 vm((chips, 8, half), F32),
+                vm((2, items // 128, 128), F32),
+                vm((tile, rows), F32),
+                vm((tile, rows), F32),
+                vm((tile, rows), BF16),
+                vm((tile, rows), BF16),
                 dma((2,)), dma((6,)), dma((6,)),
                 dma((NMSG, 2)), dma((NMSG, 2)),
                 dma((chips, 2)), dma((chips, 2)),
@@ -446,7 +489,7 @@
             ],
             compiler_params=pltpu.CompilerParams(collective_id=0, has_side_effects=True, vmem_limit_bytes=67_043_328),
         )(queries, w_first, w_second, lab, catalogue, lq)
-        return loss[0, :1], de, dw[0], dw[1].T
+        return loss, de, dw[0], dw[1].T
 
     row_spec = P(("dp", "tp"), None)
     return jax.shard_map(

time: 275 us -> 199 us (0.72)
  Pallas kernels: 264 us -> 191 us
  local copies, waits for them, and re-layouts: 9.43 us -> 5.34 us
    pallas_call x1, Pallas kernels: 264 us -> 191 us  [local_step(): pl.pallas_call(functools.partial(kernel, (n, total_rows, tile)), out_shap...]
where the time goes in v2:
time: 199 us
  Pallas kernels  191 us (96%)
  local copies, waits for them, and re-layouts  5.34 us (3%)
  between operations  2.39 us (1%)
    pallas_call x1, Pallas kernels, local_step(): pl.pallas_call(functools.partial(kernel, (n, total_rows, tile)), out_shap...  191 us

profile of v2, /device:TPU:97, one launch (start us, length us, event | category | flops | bytes accessed | tf_op | source)
XLA Modules:
  0.0 198.5 jit_solution(2607952245523917206)
XLA Ops:
  0.6 190.8 %shard_map.93 = (bf16[2048,384]{1,0:T(8,128)(2,1)}, bf16[2,384,1536]{2,1,0:T(8,128)(2,1)}, f32[1]{0:T(128)}) custom-call(bf16[256,384]{1,0:T(8,128)(2,1)} %q_ref.1, bf16[384,1536]{1,0:T(8,128)(2,1)} %w1_ref.1, bf16[1536,384]{1,0:T(8,128)(2,1)} %w2_ref.1, s32[1,256]{1,0:T(1,128)} %bitcast.9, bf16[2048,384]{1,0:T(8,128)(2,1)} %e_hbm.1, f32[16,128]{1,0:T(8,128)} %bitcast.8), custom_call_target="tpu_custom_call" | custom-call | tf_op jit(solution)/shard_map/pallas_call | solution.py:441
  191.4 2.8 %slice_bitcast_fusion = (bf16[1536,384]{0,1:T(8,128)(2,1)S(1)}, bf16[384,1536]{1,0:T(8,128)(2,1)}) fusion(bf16[2,384,1536]{2,1,0:T(8,128)(2,1)} %get-tuple-element.9), kind=kLoop, calls=%fused_computation | loop fusion | bytes 4718592 | tf_op jit(solution)/shard_map/transpose | solution.py:492
  194.2 0.0 copy-start
  194.2 1.4 copy.10
  196.2 0.0 copy-done
  196.3 1.1 copy.14
Async XLA Ops:
  194.2 2.0 %copy-start = (bf16[2048,384]{1,0:T(8,128)(2,1)S(1)}, bf16[2048,384]{1,0:T(8,128)(2,1)}, u32[]{:S(2)}) copy-start(bf16[2048,384]{1,0:T(8,128)(2,1)} %get-tuple-element.21) | copy-start | bytes 4718596

commit v3 on v2

--- a/solution.py
+++ b/solution.py
@@ -30,9 +30,9 @@
 
 
 def kernel(
-    cfg, q_ref, w1_ref, w2_ref, lab_ref, e_hbm, lq_hbm, de_out, dw_out, loss_out,
-    xg, eall, ets, lqs, act, hid, de, der, part_x, rbf, rbp, sto, sti, bco, bci, dw, dwr, pb, rwf, rwp, gb, ls, lp, lsum, lb, lqc, za, zb, ga, gbt,
-    loc_sem, d2d_s, d2d_r, ag_s, ag_r, st_s, st_r, bc_s, bc_r, rs_s, rs_r, rw_s, rw_r, gw_s, gw_r, lb_s, lb_r,
+    cfg, q_ref, w1_ref, w2_ref, lab_ref, e_hbm, lq_hbm, de_out, dw1_out, dw2_out, loss_out, gh,
+    xg, eall, ets, lqs, act, hid, de, der, part_x, rbf, rbp, sto, sti, bco, bci, dw, dwr, pb, rwf, rwp, gb, ls, lp, lsum, lb, lqc, za, zb, ga, gbt, gring, gbuf, hidt,
+    loc_sem, gr_sem, gl_sem, out_sem, d2d_s, d2d_r, de_s, de_r, gp_s, gp_r, ag_s, ag_r, st_s, st_r, bc_s, bc_r, rs_s, rs_r, rw_s, rw_r, gw_s, gw_r, lb_s, lb_r,
 ):
     n, total_rows, tile = cfg
     chips = n // 2
@@ -159,20 +159,26 @@
             lqs[pl.ds(pl.multiple_of(o * items + j * 128, 128), 128), :] = jnp.broadcast_to(row, (128, 128)).T
 
     load_e.wait()
-    send_e.wait_recv()
-
-    @pl.loop(0, ntile)
-    def _(i):
-        ets[i] = eall[pl.ds(pl.multiple_of(i * tile, tile), tile), :].T
-
     nslot = len(ORDER)
 
     def rows_of(i):
         return pl.ds(pl.multiple_of(i * tile, tile), tile)
+
+    def turned(i):
+        return lax.rem(i + core * (ntile // 2), ntile)
 
     def logits(t, i):
         lq = lqs[rows_of(i), :]
         return nt(eall[rows_of(i), :], xg[t].reshape(rows, dim)) - jnp.concatenate([lq, lq], axis=1)
+
+    def back(slot):
+        return ((-slot[0]) % SIDE, (-slot[1]) % SIDE)
+
+    def stat_copy(k, h):
+        return remote(sto.at[k, h], sti.at[POS[back(ORDER[k])], h], st_s.at[k, h], st_r.at[POS[back(ORDER[k])], h], dev(*owner_off(h, ORDER[k])))
+
+    def stat_recv(k, h):
+        return remote(sto.at[k, h], sti.at[k, h], st_s.at[k, h], st_r.at[k, h], me)
 
     def online(z_ref, carry):
         m, s = carry
@@ -180,11 +186,15 @@
         top = jnp.maximum(m, jnp.max(z, axis=0))
         return top, s * jnp.exp(m - top) + jnp.sum(jnp.exp(z - top[None]), axis=0)
 
-    za[...] = logits(0, 0)
+    za[...] = logits(0, turned(0))
 
     @pl.loop(0, nslot)
     def _(t):
         def two(i, carry):
+            @pl.when((t == 0) & (i == ntile // 4 - 1))
+            def _():
+                send_e.wait_recv()
+
             @pl.when(i == ntile // 2 - 1)
             def _():
                 for k in range(1, nslot):
@@ -192,11 +202,14 @@
                     def _(k=k):
                         x_arrived(ORDER[k])
                         x_forward(ORDER[k])
+                        if k >= 3:
+                            for h in range(2):
+                                stat_copy(k - 2, h).start()
 
             last = (2 * i + 2) // ntile
-            zb[...] = logits(t, 2 * i + 1)
+            zb[...] = logits(t, turned(2 * i + 1))
             carry = online(za, carry)
-            za[...] = logits(jnp.minimum(t + last, nslot - 1), lax.rem(2 * i + 2, ntile))
+            za[...] = logits(jnp.minimum(t + last, nslot - 1), turned(lax.rem(2 * i + 2, ntile)))
             return online(zb, carry)
 
         m, s = lax.fori_loop(0, ntile // 2, two, (jnp.full((8, rows), -jnp.inf, F32), jnp.zeros((8, rows), F32)))
@@ -207,16 +220,7 @@
             sto[t, h, 0:1, :] = top[:, lanes]
             sto[t, h, 1:2, :] = s[:, lanes]
 
-    def back(slot):
-        return ((-slot[0]) % SIDE, (-slot[1]) % SIDE)
-
-    def stat_copy(k, h):
-        return remote(sto.at[k, h], sti.at[POS[back(ORDER[k])], h], st_s.at[k, h], st_r.at[POS[back(ORDER[k])], h], dev(*owner_off(h, ORDER[k])))
-
-    def stat_recv(k, h):
-        return remote(sto.at[k, h], sti.at[k, h], st_s.at[k, h], st_r.at[k, h], me)
-
-    for k in range(1, chips):
+    for k in range(nslot - 2, nslot):
         for h in range(2):
             stat_copy(k, h).start()
     for h in range(2):
@@ -224,7 +228,9 @@
 
     @pl.loop(0, ntile)
     def _(i):
-        de[rows_of(i), :] = jnp.zeros((tile, dim), F32)
+        ets[i] = eall[rows_of(i), :].T
+
+    hidt[...] = hid[...].T
 
     @pl.loop(0, nslot)
     def _(t):
@@ -275,17 +281,24 @@
     x_settle, px_drain = reverse_tree(acc_x, box_x, add_x, rs_s, rs_r)
     first_item = chip * pair_items
 
+    ring = gring.shape[0]
+
+    def g_out(j):
+        s = j // ntile
+        return pltpu.make_async_copy(gring.at[lax.rem(j, ring)], gh.at[nslot - 1 - s, rows_of(lax.rem(j, ntile))], gr_sem.at[lax.rem(j, ring)])
+
     def soften(z_ref, g_ref, t, i):
         lse = jnp.concatenate([bci[t, 0, 0:1, :], bci[t, 1, 0:1, :]], axis=1)
         lab = jnp.concatenate([bci[t, 0, 1:2, :], bci[t, 1, 1:2, :]], axis=1).astype(jnp.int32) - (first_item + i * tile)
         z = z_ref[...] - lse
         hit = lax.broadcasted_iota(jnp.int32, (tile, rows), 0) == lab
-        g_ref[...] = (jnp.exp(z) - jnp.where(hit, 1.0 / total_rows, 0.0)).astype(BF16)
+        g = (jnp.exp(z) - jnp.where(hit, 1.0 / total_rows, 0.0)).astype(BF16)
+        g_ref[...] = g
+        gring[lax.rem((nslot - 1 - t) * ntile + i, ring)] = g
         lsum[...] += jnp.sum(jnp.where(hit, z, 0.0).reshape(tile // 8, 8, rows), axis=0)
 
     def spread(g_ref, t, i):
         g = g_ref[...]
-        de[rows_of(i), :] += nn(g, xg[t].reshape(rows, dim))
         dx = nn(ets[i], g)
         for h in range(2):
             part_x[t, h] += dx[:, h * half:(h + 1) * half]
@@ -296,6 +309,18 @@
 
         @pl.loop(0, ntile // 2)
         def _(i):
+            j = s * ntile + 2 * i
+
+            @pl.when(j >= 2)
+            def _():
+                g_out(j - 2).start()
+                g_out(j - 1).start()
+
+                @pl.when(j >= ring)
+                def _():
+                    g_out(j - ring).wait()
+                    g_out(j - ring + 1).wait()
+
             @pl.when(i == 1)
             def _():
                 for k in range(1, nslot):
@@ -313,29 +338,41 @@
             spread(ga, t, 2 * i)
 
     spread(gbt, 0, ntile - 1)
+    njob = nslot * ntile
+    g_out(njob - 2).start()
+    g_out(njob - 1).start()
+    for j in range(ring):
+        g_out(njob - ring + j).wait()
+
+    crows = gbuf.shape[2]
+    nchunk = pair_items // crows
+    hchunk = nchunk // 2
+
+    def g_in(j):
+        start = jnp.where(j < hchunk, other, core) * items + lax.rem(j, hchunk) * crows
+        slot = lax.rem(j, 2)
+        return pltpu.make_async_copy(gh.at[:, pl.ds(pl.multiple_of(start, crows), crows), :], gbuf.at[slot], gl_sem.at[slot])
+
+    g_in(0).start()
+    g_in(1).start()
     x_settle(ORDER[0])
 
-    theirs = pl.ds(pl.multiple_of(other * items, items), items)
-    send_de = remote(de.at[theirs], der, d2d_s.at[2], d2d_r.at[2], partner)
     ls[...] = lsum[:, :half] + lsum[:, half:]
     send_ls = remote(ls, lp, d2d_s.at[3], d2d_r.at[3], partner)
-    send_ls.start()
-
-    dxt = jnp.concatenate([part_x[0, 0], part_x[0, 1]], axis=1)
-    dx = dxt.T.astype(BF16)
-    dw[1] = nn(dxt.astype(BF16), hid[...])
+
+    dx = jnp.concatenate([part_x[0, 0], part_x[0, 1]], axis=1).T.astype(BF16)
     dh = nt(dx, w2_ref[...])
     da = jnp.where(act[...] > 0.0, dh, 0.0).astype(BF16)
     dw[0] = nn(q_ref[...].T, da)
+    block = dim // (2 * SIDE)
+    width = w1_ref.shape[1] // SIDE
+    for o in range(SIDE):
+        dw[1, :, o * width:(o + 1) * width] = nn(hidt[o * width:(o + 1) * width, :], dx)
+    send_ls.start()
     send_dw = remote(dw.at[other], dwr, d2d_s.at[4], d2d_r.at[4], partner)
     send_dw.start()
-    send_de.start()
-
-    send_ls.wait()
-    ls2 = lb.at[chip]
-    lsum[:, :half] = ls[...] + lp[...]
+
     lsum_src = lsum.at[:, pl.ds(0, half)]
-    ls2[...] = lsum[:, :half]
 
     def lb_copy(k):
         return remote(lsum_src, lb.at[chip], lb_s.at[k], lb_r.at[POS[back(ORDER[k])]], dev(*ORDER[k]))
@@ -343,23 +380,28 @@
     def lb_recv(k):
         return remote(lsum_src, lb.at[chip_at(*ORDER[k])], lb_s.at[k], lb_r.at[k], me)
 
-    for k in range(1, chips):
-        lb_copy(k).start()
-
-    block = dim // (2 * SIDE)
-    width = w1_ref.shape[1] // SIDE
+    def loss_step():
+        send_ls.wait()
+        both = ls[...] + lp[...]
+        lsum[:, :half] = both
+        lb[chip] = both
+
+    def loss_send():
+        for k in range(1, chips):
+            lb_copy(k).start()
 
     def where_w(k, h):
         ox, oy = owner_off(h, ORDER[k])
         r = (lax.rem(cy + oy, SIDE) * 2 + h) * block
         c = lax.rem(cx + ox, SIDE) * width
-        return pl.ds(pl.multiple_of(r, block), block), pl.ds(pl.multiple_of(c, width), width)
-
-    send_dw.wait()
-    for k in range(chips):
-        for h in range(2):
-            r, c = where_w(k, h)
-            pb[k, h] = dw[core, r, c] + dwr[r, c]
+        return pl.multiple_of(r, block), pl.multiple_of(c, width)
+
+    def pair_sum():
+        send_dw.wait()
+        for k in range(chips):
+            for h in range(2):
+                r, c = where_w(k, h)
+                pb[k, h] = dw[core, pl.ds(r, block), pl.ds(c, width)] + dwr[pl.ds(r, block), pl.ds(c, width)]
 
     lo_w = block // 2
 
@@ -375,10 +417,6 @@
         ref[...] = ref[...] + box_w(i, h)[...]
 
     w_settle, pw_drain = reverse_tree(acc_w, box_w, add_w, rw_s, rw_r)
-    for slot in reversed(ORDER):
-        w_settle(slot)
-
-    gb[core, 0] = pb[0].astype(BF16)
     cuts = (pl.ds(0, 32), pl.ds(32, block - 32))
 
     def loc_g(slot, h, part):
@@ -386,26 +424,94 @@
         return gb.at[core, k, h] if part is None else gb.at[core, k, h, cuts[part]]
 
     g_arrived, g_forward, g_drain = tree(loc_g, gw_s, gw_r)
-    g_forward((0, 0))
-
-    send_de.wait()
-    de_out[...] = (de[mine, :] + der[...]).astype(BF16)
+
+    def settle_all(*slots):
+        def act_now():
+            for slot in slots:
+                w_settle(slot)
+        return act_now
+
+    def first_sends():
+        pair_sum()
+        settle_all((2, 2), (3, 2), (1, 2), (0, 2))()
+
+    def rounded():
+        w_settle((0, 0))
+        gb[core, 0] = pb[0].astype(BF16)
+        g_forward((0, 0))
+
+    steps = {
+        1: loss_step, 2: loss_send, 3: first_sends, 5: settle_all((2, 3), (2, 1)), 6: settle_all((3, 3), (3, 1)),
+        7: settle_all((1, 3), (1, 1)), 8: settle_all((0, 3), (0, 1)), 10: settle_all((2, 0)), 12: settle_all((3, 0), (1, 0)), 14: rounded,
+    }
+
+    def de_send(j):
+        return remote(de.at[j], der.at[j], de_s.at[j], de_r.at[j], partner)
+
+    def chunk(j):
+        g_in(j).wait()
+        slot = lax.rem(j, 2)
+        return functools.reduce(jnp.add, [nn(gbuf[slot, t], xg[t].reshape(rows, dim)) for t in range(nslot)])
+
+    def at_steps(j, lo, hi):
+        for k in range(lo, hi):
+            if k in steps:
+                @pl.when(j == k)
+                def _(k=k):
+                    steps[k]()
+
+    @pl.loop(0, hchunk)
+    def _(j):
+        at_steps(j, 0, hchunk)
+
+        @pl.when(j > 0)
+        def _():
+            de_send(j - 1).start()
+
+        de[j] = chunk(j)
+        g_in(j + 2).start()
+
+    @pl.loop(hchunk, nchunk)
+    def _(j):
+        at_steps(j, hchunk, nchunk)
+
+        @pl.when(j == hchunk)
+        def _():
+            de_send(hchunk - 1).start()
+
+        own = j - hchunk
+        grad = chunk(j)
+        de_send(own).wait_recv()
+        de_out[pl.ds(pl.multiple_of(own * crows, crows), crows), :] = (grad + der[own]).astype(BF16)
+
+        @pl.when(j + 2 < nchunk)
+        def _():
+            g_in(j + 2).start()
+
+    def pair_copy(k):
+        return remote(gb.at[core, k], gb.at[core, k], gp_s.at[k], gp_r.at[k], partner)
+
+    pair_copy(0).start()
     for k in range(1, chips):
         lb_recv(k).wait_recv()
     tot = functools.reduce(jnp.add, [lb[k] for k in range(chips)])
     loss_out[0] = -jnp.sum(tot) / total_rows - math.log(total_rows)
 
-    for slot in ORDER[1:]:
-        g_arrived(slot)
-        g_forward(slot)
-    send_gb = remote(gb.at[core], gb.at[core], d2d_s.at[5], d2d_r.at[5], partner)
-    send_gb.start()
-    send_gb.wait()
-    for o in range(2):
-        for k in range(chips):
+    for k in range(1, nslot):
+        g_arrived(ORDER[k])
+        g_forward(ORDER[k])
+        pair_copy(k).start()
+
+    def out_copy(o, k, h):
+        r, c = where_w(k, h)
+        dst = dw1_out.at[pl.ds(r, block), pl.ds(c, width)] if o == 0 else dw2_out.at[pl.ds(pl.multiple_of(c + r, block), block), :]
+        return pltpu.make_async_copy(gb.at[o, k, h], dst, out_sem.at[o, k, h])
+
+    for k in range(chips):
+        pair_copy(k).wait_recv()
+        for o in range(2):
             for h in range(2):
-                r, c = where_w(k, h)
-                dw_out[o, r, c] = gb[o, k, h]
+                out_copy(o, k, h).start()
 
     send_e.wait_send()
     send_l.wait_send()
@@ -413,11 +519,19 @@
     px_drain()
     pw_drain()
     g_drain()
+    for j in range(hchunk):
+        de_send(j).wait_send()
+    for k in range(chips):
+        pair_copy(k).wait_send()
     for k in range(1, chips):
         lb_copy(k).wait_send()
         for h in range(2):
             stat_copy(k, h).wait_send()
             bc_copy(k, h).wait_send()
+    for k in range(chips):
+        for o in range(2):
+            for h in range(2):
+                out_copy(o, k, h).wait()
 
 
 def solution(mesh):
@@ -429,6 +543,8 @@
         items = catalogue.shape[0]
         total_rows = rows * n
         tile = 512
+        crows = 256
+        ring = 8
         half = rows // 2
         chips = n // 2
         lab = labels.reshape(1, rows)
@@ -438,15 +554,17 @@
         block, width = dim // (2 * SIDE), hidden // SIDE
         vspec = pl.BlockSpec(memory_space=pltpu.VMEM)
         aspec = pl.BlockSpec(memory_space=pl.ANY)
-        de, dw, loss = pl.pallas_call(
+        de, dw1, dw2, loss, _ = pl.pallas_call(
             functools.partial(kernel, (n, total_rows, tile)),
             out_shape=[
                 jax.ShapeDtypeStruct((items, dim), BF16),
-                jax.ShapeDtypeStruct((2, dim, hidden), BF16),
+                jax.ShapeDtypeStruct((dim, hidden), BF16),
+                jax.ShapeDtypeStruct((hidden, dim), BF16),
                 jax.ShapeDtypeStruct((1,), F32),
+                jax.ShapeDtypeStruct((chips, 2 * items, rows), BF16),
             ],
             in_specs=[vspec] * 4 + [aspec] * 2,
-            out_specs=[vspec] * 2 + [pl.BlockSpec(memory_space=pltpu.SMEM)],
+            out_specs=[vspec, aspec, aspec, pl.BlockSpec(memory_space=pltpu.SMEM), aspec],
             scratch_shapes=[
                 vm((chips, 2, half, dim), BF16),
                 vm((2 * items, dim), BF16),
@@ -454,8 +572,8 @@
                 vm((2 * items, 128), F32),
                 vm((rows, hidden), F32),
                 vm((rows, hidden), BF16),
-                vm((2 * items, dim), F32),
-                vm((items, dim), F32),
+                vm((items // crows, crows, dim), F32),
+                vm((items // crows, crows, dim), F32),
                 vm((chips, 2, dim, half), F32),
                 vm((len(FULL), 2, dim, half), F32),
                 vm((len(PART), 2, dim // 2, half), F32),
@@ -478,7 +596,11 @@
                 vm((tile, rows), F32),
                 vm((tile, rows), BF16),
                 vm((tile, rows), BF16),
-                dma((2,)), dma((6,)), dma((6,)),
+                vm((ring, tile, rows), BF16),
+                vm((2, chips, crows, rows), BF16),
+                vm((hidden, rows), BF16),
+                dma((2,)), dma((ring,)), dma((2,)), dma((2, chips, 2)), dma((6,)), dma((6,)),
+                dma((items // crows,)), dma((items // crows,)), dma((chips,)), dma((chips,)),
                 dma((NMSG, 2)), dma((NMSG, 2)),
                 dma((chips, 2)), dma((chips, 2)),
                 dma((chips, 2)), dma((chips, 2)),
@@ -489,7 +611,7 @@
             ],
             compiler_params=pltpu.CompilerParams(collective_id=0, has_side_effects=True, vmem_limit_bytes=67_043_328),
         )(queries, w_first, w_second, lab, catalogue, lq)
-        return loss, de, dw[0], dw[1].T
+        return loss, de, dw1, dw2
 
     row_spec = P(("dp", "tp"), None)
     return jax.shard_map(

time: 199 us -> 182 us (0.915)
  Pallas kernels: 191 us -> 174 us
    pallas_call x1, Pallas kernels: 191 us -> 174 us  [local_step(): pl.pallas_call(functools.partial(kernel, (n, total_rows, tile)), out_shap...]
    unnamed x4 -> x7, local copies, waits for them, and re-layouts: 2.55 us -> 5.52 us
    transpose x1 -> x0, local copies, waits for them, and re-layouts: 2.79 us -> none  [local_step(): return (loss, de, dw[0], dw[1].T)]
where the time goes in v3:
time: 182 us
  Pallas kernels  174 us (96%)
  local copies, waits for them, and re-layouts  5.52 us (3%)
  between operations  2.4 us (1%)
    pallas_call x1, Pallas kernels, local_step(): pl.pallas_call(functools.partial(kernel, (n, total_rows, tile)), out_shap...  174 us
    unnamed x7, local copies, waits for them, and re-layouts  5.52 us

profile of v3, /device:TPU:97, one launch (start us, length us, event | category | flops | bytes accessed | tf_op | source)
XLA Modules:
  0.0 182.1 jit_solution(15613971037449930455)
XLA Ops:
  0.6 174.2 %shard_map.93 = (bf16[2048,384]{1,0:T(8,128)(2,1)}, bf16[384,1536]{1,0:T(8,128)(2,1)}, bf16[1536,384]{1,0:T(8,128)(2,1)}, f32[1]{0:T(128)}, bf16[16,4096,256]{2,1,0:T(8,128)(2,1)}) custom-call(bf16[256,384]{1,0:T(8,128)(2,1)} %q_ref.1, bf16[384,1536]{1,0:T(8,128)(2,1)} %w1_ref.1, bf16[1536,384]{1,0:T(8,128)(2,1)} %w2_ref.1, s32[1,256]{1,0:T(1,128)} %bitcast.3, ...), custom_call_target="tpu_custom_call" | custom-call | tf_op jit(solution)/shard_map/pallas_call | solution.py:557
  175.4 0.0 copy-start.1
  175.4 2.8 %copy.15 = bf16[2048,384]{1,0:T(8,128)(2,1)} copy(bf16[2048,384]{1,0:T(8,128)(2,1)} %get-tuple-element.17) | data formatting | bytes 3145728
  178.2 0.0 copy-done.1
  178.3 0.0 copy-start
  178.3 1.0 copy.16
  179.3 0.7 copy-done
  179.9 1.0 copy.17
Async XLA Ops:
  175.4 2.8 %copy-start.1 = (bf16[384,1536]{1,0:T(8,128)(2,1)S(1)}, bf16[384,1536]{1,0:T(8,128)(2,1)}, u32[]{:S(2)}) copy-start(bf16[384,1536]{1,0:T(8,128)(2,1)} %get-tuple-element.18) | copy-start | bytes 3538948
  178.3 1.7 copy-start

commit v4 on v3

--- a/solution.py
+++ b/solution.py
@@ -32,7 +32,7 @@
 def kernel(
     cfg, q_ref, w1_ref, w2_ref, lab_ref, e_hbm, lq_hbm, de_out, dw1_out, dw2_out, loss_out, gh,
     xg, eall, ets, lqs, act, hid, de, der, part_x, rbf, rbp, sto, sti, bco, bci, dw, dwr, pb, rwf, rwp, gb, ls, lp, lsum, lb, lqc, za, zb, ga, gbt, gring, gbuf, hidt,
-    loc_sem, gr_sem, gl_sem, out_sem, d2d_s, d2d_r, de_s, de_r, gp_s, gp_r, ag_s, ag_r, st_s, st_r, bc_s, bc_r, rs_s, rs_r, rw_s, rw_r, gw_s, gw_r, lb_s, lb_r,
+    loc_sem, gr_sem, gl_sem, out_sem, d2d_s, d2d_r, de_s, de_r, gp_s, gp_r, dw_s, dw_r, ag_s, ag_r, st_s, st_r, bc_s, bc_r, rs_s, rs_r, rw_s, rw_r, gw_s, gw_r, lb_s, lb_r,
 ):
     n, total_rows, tile = cfg
     chips = n // 2
@@ -81,9 +81,11 @@
     bco[...] = jnp.zeros_like(bco)
 
     pl.semaphore_wait(barrier, len(peers) + 1)
-    send_e = remote(e_hbm, eall.at[mine], d2d_s.at[0], d2d_r.at[0], partner)
-    send_l = remote(lq_hbm, lqc.at[core], d2d_s.at[1], d2d_r.at[1], partner)
+    send_e = remote(eall.at[mine], eall.at[mine], d2d_s.at[0], d2d_r.at[0], partner)
+    send_l = remote(lqc.at[core], lqc.at[core], d2d_s.at[1], d2d_r.at[1], partner)
+    load_l.wait()
     send_l.start()
+    load_e.wait()
     send_e.start()
 
     pre = nn(q_ref[...], w1_ref[...])
@@ -148,7 +150,6 @@
     x_arrived, x_forward, x_drain = tree(loc_x, ag_s, ag_r)
     x_forward((0, 0))
 
-    load_l.wait()
     send_l.wait_recv()
 
     @pl.loop(0, 2)
@@ -158,7 +159,6 @@
             row = lqc[o, pl.ds(j, 1), :]
             lqs[pl.ds(pl.multiple_of(o * items + j * 128, 128), 128), :] = jnp.broadcast_to(row, (128, 128)).T
 
-    load_e.wait()
     nslot = len(ORDER)
 
     def rows_of(i):
@@ -190,12 +190,12 @@
 
     @pl.loop(0, nslot)
     def _(t):
-        def two(i, carry):
-            @pl.when((t == 0) & (i == ntile // 4 - 1))
+        def four(i, carry):
+            @pl.when((t == 0) & (i == ntile // 8 - 1))
             def _():
                 send_e.wait_recv()
 
-            @pl.when(i == ntile // 2 - 1)
+            @pl.when(i == ntile // 4 - 1)
             def _():
                 for k in range(1, nslot):
                     @pl.when(t == k - 1)
@@ -206,13 +206,17 @@
                             for h in range(2):
                                 stat_copy(k - 2, h).start()
 
-            last = (2 * i + 2) // ntile
-            zb[...] = logits(t, turned(2 * i + 1))
+            last = (4 * i + 4) // ntile
+            zb[...] = logits(t, turned(4 * i + 1))
             carry = online(za, carry)
-            za[...] = logits(jnp.minimum(t + last, nslot - 1), turned(lax.rem(2 * i + 2, ntile)))
+            za[...] = logits(t, turned(4 * i + 2))
+            carry = online(zb, carry)
+            zb[...] = logits(t, turned(4 * i + 3))
+            carry = online(za, carry)
+            za[...] = logits(jnp.minimum(t + last, nslot - 1), turned(lax.rem(4 * i + 4, ntile)))
             return online(zb, carry)
 
-        m, s = lax.fori_loop(0, ntile // 2, two, (jnp.full((8, rows), -jnp.inf, F32), jnp.zeros((8, rows), F32)))
+        m, s = lax.fori_loop(0, ntile // 4, four, (jnp.full((8, rows), -jnp.inf, F32), jnp.zeros((8, rows), F32)))
         top = jnp.max(m, axis=0, keepdims=True)
         s = jnp.sum(s * jnp.exp(m - top), axis=0, keepdims=True)
         for h in range(2):
@@ -226,9 +230,10 @@
     for h in range(2):
         sti[0, h] = sto[0, h]
 
-    @pl.loop(0, ntile)
+    @pl.loop(0, ntile // 2)
     def _(i):
-        ets[i] = eall[rows_of(i), :].T
+        for o in range(2):
+            ets[i, :, o * tile:(o + 1) * tile] = eall[rows_of(2 * i + o), :].T
 
     hidt[...] = hid[...].T
 
@@ -287,19 +292,18 @@
         s = j // ntile
         return pltpu.make_async_copy(gring.at[lax.rem(j, ring)], gh.at[nslot - 1 - s, rows_of(lax.rem(j, ntile))], gr_sem.at[lax.rem(j, ring)])
 
-    def soften(z_ref, g_ref, t, i):
+    def soften(z_ref, g_ref, o, t, i):
         lse = jnp.concatenate([bci[t, 0, 0:1, :], bci[t, 1, 0:1, :]], axis=1)
         lab = jnp.concatenate([bci[t, 0, 1:2, :], bci[t, 1, 1:2, :]], axis=1).astype(jnp.int32) - (first_item + i * tile)
         z = z_ref[...] - lse
         hit = lax.broadcasted_iota(jnp.int32, (tile, rows), 0) == lab
         g = (jnp.exp(z) - jnp.where(hit, 1.0 / total_rows, 0.0)).astype(BF16)
-        g_ref[...] = g
+        g_ref[o * tile:(o + 1) * tile, :] = g
         gring[lax.rem((nslot - 1 - t) * ntile + i, ring)] = g
         lsum[...] += jnp.sum(jnp.where(hit, z, 0.0).reshape(tile // 8, 8, rows), axis=0)
 
     def spread(g_ref, t, i):
-        g = g_ref[...]
-        dx = nn(ets[i], g)
+        dx = nn(ets[i], g_ref[...])
         for h in range(2):
             part_x[t, h] += dx[:, h * half:(h + 1) * half]
 
@@ -307,19 +311,19 @@
     def _(s):
         t = nslot - 1 - s
 
-        @pl.loop(0, ntile // 2)
+        @pl.loop(0, ntile // 4)
         def _(i):
-            j = s * ntile + 2 * i
-
-            @pl.when(j >= 2)
+            j = s * ntile + 4 * i
+
+            @pl.when(j >= 4)
             def _():
-                g_out(j - 2).start()
-                g_out(j - 1).start()
+                for o in range(4):
+                    g_out(j - 4 + o).start()
 
                 @pl.when(j >= ring)
                 def _():
-                    g_out(j - ring).wait()
-                    g_out(j - ring + 1).wait()
+                    for o in range(4):
+                        g_out(j - ring + o).wait()
 
             @pl.when(i == 1)
             def _():
@@ -329,18 +333,22 @@
                         x_settle(ORDER[k])
 
             first = jnp.where(i == 0, 1, 0)
-            last = (2 * i + 2) // ntile
-            zb[...] = logits(t, 2 * i + 1)
-            soften(za, ga, t, 2 * i)
-            spread(gbt, jnp.minimum(t + first, nslot - 1), lax.rem(2 * i + ntile - 1, ntile))
-            za[...] = logits(jnp.maximum(t - last, 0), lax.rem(2 * i + 2, ntile))
-            soften(zb, gbt, t, 2 * i + 1)
+            last = (4 * i + 4) // ntile
+            zb[...] = logits(t, 4 * i + 1)
+            soften(za, ga, 0, t, 4 * i)
+            spread(gbt, jnp.minimum(t + first, nslot - 1), lax.rem(2 * i + ntile // 2 - 1, ntile // 2))
+            za[...] = logits(t, 4 * i + 2)
+            soften(zb, ga, 1, t, 4 * i + 1)
+            zb[...] = logits(t, 4 * i + 3)
+            soften(za, gbt, 0, t, 4 * i + 2)
             spread(ga, t, 2 * i)
-
-    spread(gbt, 0, ntile - 1)
+            za[...] = logits(jnp.maximum(t - last, 0), lax.rem(4 * i + 4, ntile))
+            soften(zb, gbt, 1, t, 4 * i + 3)
+
+    spread(gbt, 0, ntile // 2 - 1)
     njob = nslot * ntile
-    g_out(njob - 2).start()
-    g_out(njob - 1).start()
+    for o in range(4):
+        g_out(njob - 4 + o).start()
     for j in range(ring):
         g_out(njob - ring + j).wait()
 
@@ -369,9 +377,6 @@
     for o in range(SIDE):
         dw[1, :, o * width:(o + 1) * width] = nn(hidt[o * width:(o + 1) * width, :], dx)
     send_ls.start()
-    send_dw = remote(dw.at[other], dwr, d2d_s.at[4], d2d_r.at[4], partner)
-    send_dw.start()
-
     lsum_src = lsum.at[:, pl.ds(0, half)]
 
     def lb_copy(k):
@@ -396,12 +401,20 @@
         c = lax.rem(cx + ox, SIDE) * width
         return pl.multiple_of(r, block), pl.multiple_of(c, width)
 
-    def pair_sum():
-        send_dw.wait()
-        for k in range(chips):
-            for h in range(2):
-                r, c = where_w(k, h)
-                pb[k, h] = dw[core, pl.ds(r, block), pl.ds(c, width)] + dwr[pl.ds(r, block), pl.ds(c, width)]
+    def dw_send(k, h):
+        r, c = where_w(k, h)
+        return remote(dw.at[other, pl.ds(r, block), pl.ds(c, width)], dwr.at[k, h], dw_s.at[k, h], dw_r.at[k, h], partner)
+
+    for k in reversed(range(chips)):
+        for h in range(2):
+            dw_send(k, h).start()
+
+    def pair_sum(slot):
+        k = POS[slot]
+        for h in range(2):
+            dw_send(k, h).wait_recv()
+            r, c = where_w(k, h)
+            pb[k, h] = dw[core, pl.ds(r, block), pl.ds(c, width)] + dwr[k, h]
 
     lo_w = block // 2
 
@@ -425,24 +438,31 @@
 
     g_arrived, g_forward, g_drain = tree(loc_g, gw_s, gw_r)
 
+    def pair_copy(k):
+        return remote(gb.at[core, k], gb.at[core, k], gp_s.at[k], gp_r.at[k], partner)
+
+    def onward(k):
+        g_arrived(ORDER[k])
+        g_forward(ORDER[k])
+        pair_copy(k).start()
+
     def settle_all(*slots):
         def act_now():
             for slot in slots:
+                pair_sum(slot)
                 w_settle(slot)
         return act_now
 
-    def first_sends():
-        pair_sum()
-        settle_all((2, 2), (3, 2), (1, 2), (0, 2))()
-
     def rounded():
+        pair_sum((0, 0))
         w_settle((0, 0))
         gb[core, 0] = pb[0].astype(BF16)
         g_forward((0, 0))
 
     steps = {
-        1: loss_step, 2: loss_send, 3: first_sends, 5: settle_all((2, 3), (2, 1)), 6: settle_all((3, 3), (3, 1)),
-        7: settle_all((1, 3), (1, 1)), 8: settle_all((0, 3), (0, 1)), 10: settle_all((2, 0)), 12: settle_all((3, 0), (1, 0)), 14: rounded,
+        1: settle_all((2, 2), (3, 2), (1, 2), (0, 2)), 2: loss_step, 3: settle_all((2, 3), (2, 1)), 4: settle_all((3, 3), (3, 1)),
+        5: settle_all((1, 3), (1, 1)), 6: settle_all((0, 3), (0, 1)), 7: loss_send, 8: settle_all((2, 0)), 10: settle_all((3, 0), (1, 0)), 12: rounded,
+        14: lambda: onward(1), 15: lambda: onward(2),
     }
 
     def de_send(j):
@@ -488,19 +508,14 @@
         def _():
             g_in(j + 2).start()
 
-    def pair_copy(k):
-        return remote(gb.at[core, k], gb.at[core, k], gp_s.at[k], gp_r.at[k], partner)
-
     pair_copy(0).start()
     for k in range(1, chips):
         lb_recv(k).wait_recv()
     tot = functools.reduce(jnp.add, [lb[k] for k in range(chips)])
     loss_out[0] = -jnp.sum(tot) / total_rows - math.log(total_rows)
 
-    for k in range(1, nslot):
-        g_arrived(ORDER[k])
-        g_forward(ORDER[k])
-        pair_copy(k).start()
+    for k in range(3, nslot):
+        onward(k)
 
     def out_copy(o, k, h):
         r, c = where_w(k, h)
@@ -523,6 +538,8 @@
         de_send(j).wait_send()
     for k in range(chips):
         pair_copy(k).wait_send()
+        for h in range(2):
+            dw_send(k, h).wait_send()
     for k in range(1, chips):
         lb_copy(k).wait_send()
         for h in range(2):
@@ -568,7 +585,7 @@
             scratch_shapes=[
                 vm((chips, 2, half, dim), BF16),
                 vm((2 * items, dim), BF16),
-                vm((2 * items // tile, dim, tile), BF16),
+                vm((2 * items // tile // 2, dim, 2 * tile), BF16),
                 vm((2 * items, 128), F32),
                 vm((rows, hidden), F32),
                 vm((rows, hidden), BF16),
@@ -582,7 +599,7 @@
                 vm((2, 8, half), F32),
                 vm((chips, 2, 8, half), F32),
                 vm((2, dim, hidden), F32),
-                vm((dim, hidden), F32),
+                vm((chips, 2, block, width), F32),
                 vm((chips, 2, block, width), F32),
                 vm((len(FULL), 2, block, width), F32),
                 vm((len(PART), 2, block // 2, width), F32),
@@ -594,13 +611,13 @@
                 vm((2, items // 128, 128), F32),
                 vm((tile, rows), F32),
                 vm((tile, rows), F32),
-                vm((tile, rows), BF16),
-                vm((tile, rows), BF16),
+                vm((2 * tile, rows), BF16),
+                vm((2 * tile, rows), BF16),
                 vm((ring, tile, rows), BF16),
                 vm((2, chips, crows, rows), BF16),
                 vm((hidden, rows), BF16),
                 dma((2,)), dma((ring,)), dma((2,)), dma((2, chips, 2)), dma((6,)), dma((6,)),
-                dma((items // crows,)), dma((items // crows,)), dma((chips,)), dma((chips,)),
+                dma((items // crows,)), dma((items // crows,)), dma((chips,)), dma((chips,)), dma((chips, 2)), dma((chips, 2)),
                 dma((NMSG, 2)), dma((NMSG, 2)),
                 dma((chips, 2)), dma((chips, 2)),
                 dma((chips, 2)), dma((chips, 2)),

time: 182 us -> 171 us (0.940)
  Pallas kernels: 174 us -> 163 us
    pallas_call x1, Pallas kernels: 174 us -> 163 us  [local_step(): pl.pallas_call(functools.partial(kernel, (n, total_rows, tile)), out_shap...]
where the time goes in v4:
time: 171 us
  Pallas kernels  163 us (95%)
  local copies, waits for them, and re-layouts  5.52 us (3%)
  between operations  2.4 us (1%)
    pallas_call x1, Pallas kernels, local_step(): pl.pallas_call(functools.partial(kernel, (n, total_rows, tile)), out_shap...  163 us
    unnamed x7, local copies, waits for them, and re-layouts  5.52 us

profile of v4, /device:TPU:97, one launch (start us, length us, event | category | flops | bytes accessed | tf_op | source)
XLA Modules:
  0.0 170.6 jit_solution(2486636863659987188)
XLA Ops:
  0.6 162.7 %shard_map.93 = (bf16[2048,384]{1,0:T(8,128)(2,1)}, bf16[384,1536]{1,0:T(8,128)(2,1)}, bf16[1536,384]{1,0:T(8,128)(2,1)}, f32[1]{0:T(128)}, bf16[16,4096,256]{2,1,0:T(8,128)(2,1)}) custom-call(bf16[256,384]{1,0:T(8,128)(2,1)} %q_ref.1, bf16[384,1536]{1,0:T(8,128)(2,1)} %w1_ref.1, bf16[1536,384]{1,0:T(8,128)(2,1)} %w2_ref.1, s32[1,256]{1,0:T(1,128)} %bitcast.3, ...), custom_call_target="tpu_custom_call" | custom-call | tf_op jit(solution)/shard_map/pallas_call | solution.py:574
  163.9 0.0 copy-start.1
  163.9 2.8 %copy.15 = bf16[2048,384]{1,0:T(8,128)(2,1)} copy(bf16[2048,384]{1,0:T(8,128)(2,1)} %get-tuple-element.17) | data formatting | bytes 3145728
  166.7 0.0 copy-done.1
  166.7 0.0 copy-start
  166.8 1.0 copy.16
  167.8 0.7 copy-done
  168.4 1.0 copy.17
Async XLA Ops:
  163.9 2.8 %copy-start.1 = (bf16[384,1536]{1,0:T(8,128)(2,1)S(1)}, bf16[384,1536]{1,0:T(8,128)(2,1)}, u32[]{:S(2)}) copy-start(bf16[384,1536]{1,0:T(8,128)(2,1)} %get-tuple-element.18) | copy-start | bytes 3538948
  166.7 1.7 copy-start

commit v5 on v4

--- a/solution.py
+++ b/solution.py
@@ -167,9 +167,16 @@
     def turned(i):
         return lax.rem(i + core * (ntile // 2), ntile)
 
-    def logits(t, i):
-        lq = lqs[rows_of(i), :]
-        return nt(eall[rows_of(i), :], xg[t].reshape(rows, dim)) - jnp.concatenate([lq, lq], axis=1)
+    part = 64
+
+    def chunks():
+        return [slice(r, r + part) for r in range(0, tile, part)]
+
+    def logits(z_ref, t, i):
+        z = nt(eall[rows_of(i), :], xg[t].reshape(rows, dim))
+        for r in chunks():
+            lq = lqs[pl.ds(pl.multiple_of(i * tile + r.start, part), part), :]
+            z_ref[r, :] = z[r, :] - jnp.concatenate([lq, lq], axis=1)
 
     def back(slot):
         return ((-slot[0]) % SIDE, (-slot[1]) % SIDE)
@@ -182,11 +189,15 @@
 
     def online(z_ref, carry):
         m, s = carry
-        z = z_ref[...].reshape(tile // 8, 8, rows)
-        top = jnp.maximum(m, jnp.max(z, axis=0))
-        return top, s * jnp.exp(m - top) + jnp.sum(jnp.exp(z - top[None]), axis=0)
-
-    za[...] = logits(0, turned(0))
+        top = m
+        for r in chunks():
+            top = jnp.maximum(top, jnp.max(z_ref[r, :].reshape(part // 8, 8, rows), axis=0))
+        s = s * jnp.exp(m - top)
+        for r in chunks():
+            s = s + jnp.sum(jnp.exp(z_ref[r, :].reshape(part // 8, 8, rows) - top[None]), axis=0)
+        return top, s
+
+    logits(za, 0, turned(0))
 
     @pl.loop(0, nslot)
     def _(t):
@@ -207,13 +218,13 @@
                                 stat_copy(k - 2, h).start()
 
             last = (4 * i + 4) // ntile
-            zb[...] = logits(t, turned(4 * i + 1))
+            logits(zb, t, turned(4 * i + 1))
             carry = online(za, carry)
-            za[...] = logits(t, turned(4 * i + 2))
+            logits(za, t, turned(4 * i + 2))
             carry = online(zb, carry)
-            zb[...] = logits(t, turned(4 * i + 3))
+            logits(zb, t, turned(4 * i + 3))
             carry = online(za, carry)
-            za[...] = logits(jnp.minimum(t + last, nslot - 1), turned(lax.rem(4 * i + 4, ntile)))
+            logits(za, jnp.minimum(t + last, nslot - 1), turned(lax.rem(4 * i + 4, ntile)))
             return online(zb, carry)
 
         m, s = lax.fori_loop(0, ntile // 4, four, (jnp.full((8, rows), -jnp.inf, F32), jnp.zeros((8, rows), F32)))
@@ -265,7 +276,7 @@
         for h in range(2):
             bc_copy(k, h).start()
 
-    za[...] = logits(nslot - 1, 0)
+    logits(za, nslot - 1, 0)
     for k in range(1, chips):
         for h in range(2):
             bc_recv(k, h).wait_recv()
@@ -293,19 +304,26 @@
         return pltpu.make_async_copy(gring.at[lax.rem(j, ring)], gh.at[nslot - 1 - s, rows_of(lax.rem(j, ntile))], gr_sem.at[lax.rem(j, ring)])
 
     def soften(z_ref, g_ref, o, t, i):
+        slot = lax.rem((nslot - 1 - t) * ntile + i, ring)
         lse = jnp.concatenate([bci[t, 0, 0:1, :], bci[t, 1, 0:1, :]], axis=1)
         lab = jnp.concatenate([bci[t, 0, 1:2, :], bci[t, 1, 1:2, :]], axis=1).astype(jnp.int32) - (first_item + i * tile)
-        z = z_ref[...] - lse
-        hit = lax.broadcasted_iota(jnp.int32, (tile, rows), 0) == lab
-        g = (jnp.exp(z) - jnp.where(hit, 1.0 / total_rows, 0.0)).astype(BF16)
-        g_ref[o * tile:(o + 1) * tile, :] = g
-        gring[lax.rem((nslot - 1 - t) * ntile + i, ring)] = g
-        lsum[...] += jnp.sum(jnp.where(hit, z, 0.0).reshape(tile // 8, 8, rows), axis=0)
+        lab = lab - lax.broadcasted_iota(jnp.int32, (8, rows), 0)
+        acc = jnp.zeros((8, rows), F32)
+        for r in chunks():
+            z = z_ref[r, :].reshape(part // 8, 8, rows) - lse[None]
+            at = lax.broadcasted_iota(jnp.int32, (part // 8, 8, rows), 0) * 8 + r.start
+            once = jnp.where(at == lab[None], 1.0 / total_rows, 0.0)
+            g = (jnp.exp(z) - once).reshape(part, rows).astype(BF16)
+            acc = acc + jnp.sum(once * z, axis=0)
+            g_ref[o * tile + r.start:o * tile + r.stop, :] = g
+            gring[slot, r, :] = g
+        lsum[...] += acc
 
     def spread(g_ref, t, i):
         dx = nn(ets[i], g_ref[...])
-        for h in range(2):
-            part_x[t, h] += dx[:, h * half:(h + 1) * half]
+        for r in range(0, dim, part):
+            for h in range(2):
+                part_x[t, h, r:r + part, :] += dx[r:r + part, h * half:(h + 1) * half]
 
     @pl.loop(0, nslot)
     def _(s):
@@ -334,15 +352,15 @@
 
             first = jnp.where(i == 0, 1, 0)
             last = (4 * i + 4) // ntile
-            zb[...] = logits(t, 4 * i + 1)
+            logits(zb, t, 4 * i + 1)
             soften(za, ga, 0, t, 4 * i)
             spread(gbt, jnp.minimum(t + first, nslot - 1), lax.rem(2 * i + ntile // 2 - 1, ntile // 2))
-            za[...] = logits(t, 4 * i + 2)
+            logits(za, t, 4 * i + 2)
             soften(zb, ga, 1, t, 4 * i + 1)
-            zb[...] = logits(t, 4 * i + 3)
+            logits(zb, t, 4 * i + 3)
             soften(za, gbt, 0, t, 4 * i + 2)
             spread(ga, t, 2 * i)
-            za[...] = logits(jnp.maximum(t - last, 0), lax.rem(4 * i + 4, ntile))
+            logits(za, jnp.maximum(t - last, 0), lax.rem(4 * i + 4, ntile))
             soften(zb, gbt, 1, t, 4 * i + 3)
 
     spread(gbt, 0, ntile // 2 - 1)
@@ -512,7 +530,7 @@
     for k in range(1, chips):
         lb_recv(k).wait_recv()
     tot = functools.reduce(jnp.add, [lb[k] for k in range(chips)])
-    loss_out[0] = -jnp.sum(tot) / total_rows - math.log(total_rows)
+    loss_out[0] = -jnp.sum(tot) - math.log(total_rows)
 
     for k in range(3, nslot):
         onward(k)

time: 171 us -> 165 us (0.965)
  Pallas kernels: 163 us -> 156 us
    pallas_call x1, Pallas kernels: 163 us -> 156 us  [local_step(): pl.pallas_call(functools.partial(kernel, (n, total_rows, tile)), out_shap...]
where the time goes in v5:
time: 165 us; the launch traced here: 164 us
  Pallas kernels  156 us (95%)
  local copies, waits for them, and re-layouts  5.52 us (3%)
  between operations  2.4 us (1%)
    pallas_call x1, Pallas kernels, local_step(): pl.pallas_call(functools.partial(kernel, (n, total_rows, tile)), out_shap...  156 us
    unnamed x7, local copies, waits for them, and re-layouts  5.52 us

profile of v5, /device:TPU:97, one launch (start us, length us, event | category | flops | bytes accessed | tf_op | source)
XLA Modules:
  0.0 164.4 jit_solution(1864442575747424926)
XLA Ops:
  0.6 156.5 %shard_map.93 = (bf16[2048,384]{1,0:T(8,128)(2,1)}, bf16[384,1536]{1,0:T(8,128)(2,1)}, bf16[1536,384]{1,0:T(8,128)(2,1)}, f32[1]{0:T(128)}, bf16[16,4096,256]{2,1,0:T(8,128)(2,1)}) custom-call(bf16[256,384]{1,0:T(8,128)(2,1)} %q_ref.1, bf16[384,1536]{1,0:T(8,128)(2,1)} %w1_ref.1, bf16[1536,384]{1,0:T(8,128)(2,1)} %w2_ref.1, s32[1,256]{1,0:T(1,128)} %bitcast.3, ...), custom_call_target="tpu_custom_call" | custom-call | tf_op jit(solution)/shard_map/pallas_call | solution.py:592
  157.7 0.0 copy-start.1
  157.7 2.8 %copy.15 = bf16[2048,384]{1,0:T(8,128)(2,1)} copy(bf16[2048,384]{1,0:T(8,128)(2,1)} %get-tuple-element.17) | data formatting | bytes 3145728
  160.5 0.0 copy-done.1
  160.5 0.0 copy-start
  160.5 1.0 copy.16
  161.6 0.7 copy-done
  162.2 1.0 copy.17
Async XLA Ops:
  157.7 2.8 %copy-start.1 = (bf16[384,1536]{1,0:T(8,128)(2,1)S(1)}, bf16[384,1536]{1,0:T(8,128)(2,1)}, u32[]{:S(2)}) copy-start(bf16[384,1536]{1,0:T(8,128)(2,1)} %get-tuple-element.18) | copy-start | bytes 3538948
  160.5 1.7 %copy-start = (bf16[1536,384]{1,0:T(8,128)(2,1)S(1)}, bf16[1536,384]{1,0:T(8,128)(2,1)}, u32[]{:S(2)}) copy-start(bf16[1536,384]{1,0:T(8,128)(2,1)} %get-tuple-element.19) | copy-start | bytes 3538948

commit v6 on v5

--- a/solution.py
+++ b/solution.py
@@ -16,9 +16,29 @@
 for _u in range(SIDE):
     MESSAGES += [((_u, 0), (_u, 1), None, 1, -1), ((_u, 0), (_u, 3), None, 1, 1), ((_u, 1), (_u, 2), 0, 1, -1), ((_u, 3), (_u, 2), 1, 1, 1)]
 NMSG = len(MESSAGES)
+NEAR = 4
+SOLO = (len(ORDER) - NEAR) // 2
 FULL = [i for i, msg in enumerate(MESSAGES) if msg[2] is None]
 PART = [i for i, msg in enumerate(MESSAGES) if msg[2] is not None]
 BF16, F32 = jnp.bfloat16, jnp.float32
+
+
+def blocks_of(t):
+    if isinstance(t, int):
+        if t < NEAR:
+            return (t, 0), (t, 1)
+        h = (t - NEAR) // SOLO
+        k = NEAR + 2 * (t - NEAR - h * SOLO)
+        return (k, h), (k + 1, h)
+    solo = t >= NEAR
+    h = jnp.where(t >= NEAR + SOLO, 1, 0)
+    k = NEAR + 2 * (t - NEAR - h * SOLO)
+    return (jnp.where(solo, k, t), h), (jnp.where(solo, k + 1, t), jnp.where(solo, h, 1))
+
+
+def backward_step(s):
+    last = len(ORDER) - 1
+    return jnp.where(s < SOLO, last - SOLO - s, jnp.where(s < 2 * SOLO, last + SOLO - s, last - s))
 
 
 def nt(a, b):
@@ -99,16 +119,16 @@
             src, dst, part, axis, step = MESSAGES[i]
             return remote(loc(src, h, part), loc(dst, h, part), ssem.at[i, h], rsem.at[i, h], along(h, axis, step))
 
-        def arrived(slot):
+        def arrived(slot, halves=(0, 1)):
             for i, msg in enumerate(MESSAGES):
                 if msg[1] == slot:
-                    for h in range(2):
+                    for h in halves:
                         copy(i, h).wait_recv()
 
-        def forward(slot):
+        def forward(slot, halves=(0, 1)):
             for i, msg in enumerate(MESSAGES):
                 if msg[0] == slot:
-                    for h in range(2):
+                    for h in halves:
                         copy(i, h).start()
 
         def drain():
@@ -123,15 +143,15 @@
             src, dst, part, axis, step = MESSAGES[i]
             return remote(acc(dst, h, part), box(i, h), ssem.at[i, h], rsem.at[i, h], along(h, axis, -step))
 
-        def settle(slot):
+        def settle(slot, halves=(0, 1)):
             for i, msg in enumerate(MESSAGES):
                 if msg[0] == slot:
-                    for h in range(2):
+                    for h in halves:
                         copy(i, h).wait_recv()
                         add(i, h)
             for i, msg in enumerate(MESSAGES):
                 if msg[1] == slot:
-                    for h in range(2):
+                    for h in halves:
                         copy(i, h).start()
 
         def drain():
@@ -164,6 +184,10 @@
     def rows_of(i):
         return pl.ds(pl.multiple_of(i * tile, tile), tile)
 
+    def x_of(t):
+        (k0, h0), (k1, h1) = blocks_of(t)
+        return jnp.concatenate([xg[k0, h0], xg[k1, h1]], axis=0)
+
     def turned(i):
         return lax.rem(i + core * (ntile // 2), ntile)
 
@@ -173,7 +197,7 @@
         return [slice(r, r + part) for r in range(0, tile, part)]
 
     def logits(z_ref, t, i):
-        z = nt(eall[rows_of(i), :], xg[t].reshape(rows, dim))
+        z = nt(eall[rows_of(i), :], x_of(t))
         for r in chunks():
             lq = lqs[pl.ds(pl.multiple_of(i * tile + r.start, part), part), :]
             z_ref[r, :] = z[r, :] - jnp.concatenate([lq, lq], axis=1)
@@ -197,6 +221,55 @@
             s = s + jnp.sum(jnp.exp(z_ref[r, :].reshape(part // 8, 8, rows) - top[None]), axis=0)
         return top, s
 
+    ahead = {}
+    early = [k for k in range(NEAR, nslot) if ORDER[k][1] != 2]
+    for n_, k in enumerate(early):
+        ahead.setdefault(NEAR + 2 + n_ // 2, []).append(k)
+
+    def arrivals(t):
+        if t < NEAR + SOLO:
+            for k, h in blocks_of(t):
+                x_arrived(ORDER[k], (h,))
+                x_forward(ORDER[k], (h,))
+        else:
+            for k, h in blocks_of(t):
+                if k not in early:
+                    x_arrived(ORDER[k], (h,))
+        for k in ahead.get(t, ()):
+            x_arrived(ORDER[k], (1,))
+            x_forward(ORDER[k], (1,))
+        if t == NEAR + 2 * SOLO - 2:
+            combine(0)
+
+    def stats_out(t):
+        for k, h in blocks_of(t):
+            if k > 0:
+                stat_copy(k, h).start()
+
+    def bc_copy(k, h):
+        return remote(bco.at[h], bci.at[POS[back(ORDER[k])], h], bc_s.at[k, h], bc_r.at[POS[back(ORDER[k])], h], dev(*owner_off(h, ORDER[k])))
+
+    def bc_recv(k, h):
+        return remote(bco.at[h], bci.at[k, h], bc_s.at[k, h], bc_r.at[k, h], me)
+
+    def combine(h):
+        sti[0, h] = sto[0, h]
+        for k in range(1, chips):
+            stat_recv(k, h).wait_recv()
+        tops = [sti[k, h, 0:1, :] for k in range(chips)]
+        sums = [sti[k, h, 1:2, :] for k in range(chips)]
+        top = functools.reduce(jnp.maximum, tops)
+        s = functools.reduce(jnp.add, [sm * jnp.exp(tp - top) for tp, sm in zip(tops, sums)])
+        bco[h, 0:1, :] = top + jnp.log(s) + math.log(total_rows)
+        bco[h, 1:2, :] = lab_ref[0:1, h * half:(h + 1) * half].astype(F32)
+        bci[0, h] = bco[h]
+        for k in range(1, chips):
+            bc_copy(k, h).start()
+
+    def broadcast_in(h):
+        for k in range(1, chips):
+            bc_recv(k, h).wait_recv()
+
     logits(za, 0, turned(0))
 
     @pl.loop(0, nslot)
@@ -211,11 +284,14 @@
                 for k in range(1, nslot):
                     @pl.when(t == k - 1)
                     def _(k=k):
-                        x_arrived(ORDER[k])
-                        x_forward(ORDER[k])
-                        if k >= 3:
-                            for h in range(2):
-                                stat_copy(k - 2, h).start()
+                        arrivals(k)
+
+            @pl.when(i == 0)
+            def _():
+                for k in range(1, nslot):
+                    @pl.when(t == k)
+                    def _(k=k):
+                        stats_out(k - 1)
 
             last = (4 * i + 4) // ntile
             logits(zb, t, turned(4 * i + 1))
@@ -230,16 +306,12 @@
         m, s = lax.fori_loop(0, ntile // 4, four, (jnp.full((8, rows), -jnp.inf, F32), jnp.zeros((8, rows), F32)))
         top = jnp.max(m, axis=0, keepdims=True)
         s = jnp.sum(s * jnp.exp(m - top), axis=0, keepdims=True)
-        for h in range(2):
-            lanes = slice(h * half, (h + 1) * half)
-            sto[t, h, 0:1, :] = top[:, lanes]
-            sto[t, h, 1:2, :] = s[:, lanes]
-
-    for k in range(nslot - 2, nslot):
-        for h in range(2):
-            stat_copy(k, h).start()
-    for h in range(2):
-        sti[0, h] = sto[0, h]
+        for c, (k, h) in enumerate(blocks_of(t)):
+            lanes = slice(c * half, (c + 1) * half)
+            sto[k, h, 0:1, :] = top[:, lanes]
+            sto[k, h, 1:2, :] = s[:, lanes]
+
+    stats_out(nslot - 1)
 
     @pl.loop(0, ntile // 2)
     def _(i):
@@ -254,32 +326,8 @@
 
     lsum[...] = jnp.zeros_like(lsum)
     gbt[...] = jnp.zeros_like(gbt)
-    for k in range(1, chips):
-        for h in range(2):
-            stat_recv(k, h).wait_recv()
-    for h in range(2):
-        tops = [sti[k, h, 0:1, :] for k in range(chips)]
-        sums = [sti[k, h, 1:2, :] for k in range(chips)]
-        top = functools.reduce(jnp.maximum, tops)
-        s = functools.reduce(jnp.add, [sm * jnp.exp(tp - top) for tp, sm in zip(tops, sums)])
-        bco[h, 0:1, :] = top + jnp.log(s) + math.log(total_rows)
-        bco[h, 1:2, :] = lab_ref[0:1, h * half:(h + 1) * half].astype(F32)
-        bci[0, h] = bco[h]
-
-    def bc_copy(k, h):
-        return remote(bco.at[h], bci.at[POS[back(ORDER[k])], h], bc_s.at[k, h], bc_r.at[POS[back(ORDER[k])], h], dev(*owner_off(h, ORDER[k])))
-
-    def bc_recv(k, h):
-        return remote(bco.at[h], bci.at[k, h], bc_s.at[k, h], bc_r.at[k, h], me)
-
-    for k in range(1, chips):
-        for h in range(2):
-            bc_copy(k, h).start()
-
-    logits(za, nslot - 1, 0)
-    for k in range(1, chips):
-        for h in range(2):
-            bc_recv(k, h).wait_recv()
+    logits(za, nslot - 1 - SOLO, 0)
+    broadcast_in(0)
 
     lo_x = dim // 2
 
@@ -301,12 +349,13 @@
 
     def g_out(j):
         s = j // ntile
-        return pltpu.make_async_copy(gring.at[lax.rem(j, ring)], gh.at[nslot - 1 - s, rows_of(lax.rem(j, ntile))], gr_sem.at[lax.rem(j, ring)])
-
-    def soften(z_ref, g_ref, o, t, i):
-        slot = lax.rem((nslot - 1 - t) * ntile + i, ring)
-        lse = jnp.concatenate([bci[t, 0, 0:1, :], bci[t, 1, 0:1, :]], axis=1)
-        lab = jnp.concatenate([bci[t, 0, 1:2, :], bci[t, 1, 1:2, :]], axis=1).astype(jnp.int32) - (first_item + i * tile)
+        return pltpu.make_async_copy(gring.at[lax.rem(j, ring)], gh.at[backward_step(s), rows_of(lax.rem(j, ntile))], gr_sem.at[lax.rem(j, ring)])
+
+    def soften(z_ref, g_ref, o, s, i):
+        slot = lax.rem(s * ntile + i, ring)
+        (k0, h0), (k1, h1) = blocks_of(backward_step(s))
+        lse = jnp.concatenate([bci[k0, h0, 0:1, :], bci[k1, h1, 0:1, :]], axis=1)
+        lab = jnp.concatenate([bci[k0, h0, 1:2, :], bci[k1, h1, 1:2, :]], axis=1).astype(jnp.int32) - (first_item + i * tile)
         lab = lab - lax.broadcasted_iota(jnp.int32, (8, rows), 0)
         acc = jnp.zeros((8, rows), F32)
         for r in chunks():
@@ -319,16 +368,20 @@
             gring[slot, r, :] = g
         lsum[...] += acc
 
-    def spread(g_ref, t, i):
+    def spread(g_ref, s, i):
         dx = nn(ets[i], g_ref[...])
         for r in range(0, dim, part):
-            for h in range(2):
-                part_x[t, h, r:r + part, :] += dx[r:r + part, h * half:(h + 1) * half]
+            for c, (k, h) in enumerate(blocks_of(backward_step(s))):
+                part_x[k, h, r:r + part, :] += dx[r:r + part, c * half:(c + 1) * half]
+
+    def settle_step(t):
+        for k, h in reversed(blocks_of(t)):
+            x_settle(ORDER[k], (h,))
+
+    order2 = [int(x) for x in [*range(nslot - 1 - SOLO, NEAR - 1, -1), *range(nslot - 1, nslot - 1 - SOLO, -1), *range(NEAR - 1, -1, -1)]]
 
     @pl.loop(0, nslot)
     def _(s):
-        t = nslot - 1 - s
-
         @pl.loop(0, ntile // 4)
         def _(i):
             j = s * ntile + 4 * i
@@ -346,24 +399,28 @@
             @pl.when(i == 1)
             def _():
                 for k in range(1, nslot):
-                    @pl.when(t + 1 == k)
+                    @pl.when(s == k)
                     def _(k=k):
-                        x_settle(ORDER[k])
+                        settle_step(order2[k - 1])
+                        if k == 2:
+                            combine(1)
+                        if k == SOLO - 1:
+                            broadcast_in(1)
 
             first = jnp.where(i == 0, 1, 0)
             last = (4 * i + 4) // ntile
-            logits(zb, t, 4 * i + 1)
-            soften(za, ga, 0, t, 4 * i)
-            spread(gbt, jnp.minimum(t + first, nslot - 1), lax.rem(2 * i + ntile // 2 - 1, ntile // 2))
-            logits(za, t, 4 * i + 2)
-            soften(zb, ga, 1, t, 4 * i + 1)
-            logits(zb, t, 4 * i + 3)
-            soften(za, gbt, 0, t, 4 * i + 2)
-            spread(ga, t, 2 * i)
-            logits(za, jnp.maximum(t - last, 0), lax.rem(4 * i + 4, ntile))
-            soften(zb, gbt, 1, t, 4 * i + 3)
-
-    spread(gbt, 0, ntile // 2 - 1)
+            logits(zb, backward_step(s), 4 * i + 1)
+            soften(za, ga, 0, s, 4 * i)
+            spread(gbt, jnp.maximum(s - first, 0), lax.rem(2 * i + ntile // 2 - 1, ntile // 2))
+            logits(za, backward_step(s), 4 * i + 2)
+            soften(zb, ga, 1, s, 4 * i + 1)
+            logits(zb, backward_step(s), 4 * i + 3)
+            soften(za, gbt, 0, s, 4 * i + 2)
+            spread(ga, s, 2 * i)
+            logits(za, backward_step(jnp.minimum(s + last, nslot - 1)), lax.rem(4 * i + 4, ntile))
+            soften(zb, gbt, 1, s, 4 * i + 3)
+
+    spread(gbt, nslot - 1, ntile // 2 - 1)
     njob = nslot * ntile
     for o in range(4):
         g_out(njob - 4 + o).start()
@@ -489,7 +546,7 @@
     def chunk(j):
         g_in(j).wait()
         slot = lax.rem(j, 2)
-        return functools.reduce(jnp.add, [nn(gbuf[slot, t], xg[t].reshape(rows, dim)) for t in range(nslot)])
+        return functools.reduce(jnp.add, [nn(gbuf[slot, t], x_of(t)) for t in range(nslot)])
 
     def at_steps(j, lo, hi):
         for k in range(lo, hi):

time: 165 us -> 167 us (1.012)
  Pallas kernels: 156 us -> 159 us
    pallas_call x1, Pallas kernels: 156 us -> 159 us  [local_step(): pl.pallas_call(functools.partial(kernel, (n, total_rows, tile)), out_shap...]
where the time goes in v6:
time: 167 us
  Pallas kernels  159 us (95%)
  local copies, waits for them, and re-layouts  5.52 us (3%)
  between operations  2.4 us (1%)
    pallas_call x1, Pallas kernels, local_step(): pl.pallas_call(functools.partial(kernel, (n, total_rows, tile)), out_shap...  159 us
    unnamed x7, local copies, waits for them, and re-layouts  5.52 us

profile of v6, /device:TPU:97, one launch (start us, length us, event | category | flops | bytes accessed | tf_op | source)
XLA Modules:
  0.0 167.1 jit_solution(6891843269158121804)
XLA Ops:
  0.6 159.2 %shard_map.93 = (bf16[2048,384]{1,0:T(8,128)(2,1)}, bf16[384,1536]{1,0:T(8,128)(2,1)}, bf16[1536,384]{1,0:T(8,128)(2,1)}, f32[1]{0:T(128)}, bf16[16,4096,256]{2,1,0:T(8,128)(2,1)}) custom-call(bf16[256,384]{1,0:T(8,128)(2,1)} %q_ref.1, bf16[384,1536]{1,0:T(8,128)(2,1)} %w1_ref.1, bf16[1536,384]{1,0:T(8,128)(2,1)} %w2_ref.1, s32[1,256]{1,0:T(1,128)} %bitcast.3, ...), custom_call_target="tpu_custom_call" | custom-call | tf_op jit(solution)/shard_map/pallas_call | solution.py:649
  160.5 0.0 copy-start.1
  160.5 2.8 %copy.15 = bf16[2048,384]{1,0:T(8,128)(2,1)} copy(bf16[2048,384]{1,0:T(8,128)(2,1)} %get-tuple-element.17) | data formatting | bytes 3145728
  163.3 0.0 copy-done.1
  163.3 0.0 copy-start
  163.3 1.0 copy.16
  164.3 0.7 copy-done
  165.0 1.0 copy.17
Async XLA Ops:
  160.5 2.8 %copy-start.1 = (bf16[384,1536]{1,0:T(8,128)(2,1)S(1)}, bf16[384,1536]{1,0:T(8,128)(2,1)}, u32[]{:S(2)}) copy-start(bf16[384,1536]{1,0:T(8,128)(2,1)} %get-tuple-element.18) | copy-start | bytes 3538948
  163.3 1.7 %copy-start = (bf16[1536,384]{1,0:T(8,128)(2,1)S(1)}, bf16[1536,384]{1,0:T(8,128)(2,1)}, u32[]{:S(2)}) copy-start(bf16[1536,384]{1,0:T(8,128)(2,1)} %get-tuple-element.19) | copy-start | bytes 3538948

commit v7 on v6

--- a/solution.py
+++ b/solution.py
@@ -16,7 +16,7 @@
 for _u in range(SIDE):
     MESSAGES += [((_u, 0), (_u, 1), None, 1, -1), ((_u, 0), (_u, 3), None, 1, 1), ((_u, 1), (_u, 2), 0, 1, -1), ((_u, 3), (_u, 2), 1, 1, 1)]
 NMSG = len(MESSAGES)
-NEAR = 4
+NEAR = 8
 SOLO = (len(ORDER) - NEAR) // 2
 FULL = [i for i, msg in enumerate(MESSAGES) if msg[2] is None]
 PART = [i for i, msg in enumerate(MESSAGES) if msg[2] is not None]
@@ -50,9 +50,9 @@
 
 
 def kernel(
-    cfg, q_ref, w1_ref, w2_ref, lab_ref, e_hbm, lq_hbm, de_out, dw1_out, dw2_out, loss_out, gh,
-    xg, eall, ets, lqs, act, hid, de, der, part_x, rbf, rbp, sto, sti, bco, bci, dw, dwr, pb, rwf, rwp, gb, ls, lp, lsum, lb, lqc, za, zb, ga, gbt, gring, gbuf, hidt,
-    loc_sem, gr_sem, gl_sem, out_sem, d2d_s, d2d_r, de_s, de_r, gp_s, gp_r, dw_s, dw_r, ag_s, ag_r, st_s, st_r, bc_s, bc_r, rs_s, rs_r, rw_s, rw_r, gw_s, gw_r, lb_s, lb_r,
+    cfg, q_ref, lab_ref, w1_hbm, w2_hbm, e_hbm, lq_hbm, de_hbm, dw1_out, dw2_out, loss_out, gh,
+    xg, eall, ets, lqs, act, hid, de, der, part_x, rbf, rbp, sto, sti, bco, bci, dw, dwr, pb, rwf, rwp, gb, ls, lp, lsum, lb, lqc, za, zb, ga, gbt, gring, gbuf, hidt, w1_ref, w2_ref, de_out,
+    loc_sem, deo_sem, gr_sem, gl_sem, out_sem, d2d_s, d2d_r, de_s, de_r, gp_s, gp_r, dw_s, dw_r, ag_s, ag_r, st_s, st_r, bc_s, bc_r, rs_s, rs_r, rw_s, rw_r, gw_s, gw_r, lb_s, lb_r,
 ):
     n, total_rows, tile = cfg
     chips = n // 2
@@ -96,6 +96,10 @@
     load_l = pltpu.make_async_copy(lq_hbm, lqc.at[core], loc_sem.at[1])
     load_e.start()
     load_l.start()
+    load_w1 = pltpu.make_async_copy(w1_hbm, w1_ref, loc_sem.at[2])
+    load_w2 = pltpu.make_async_copy(w2_hbm, w2_ref, loc_sem.at[3])
+    load_w1.start()
+    load_w2.start()
 
     sto[...] = jnp.zeros_like(sto)
     bco[...] = jnp.zeros_like(bco)
@@ -108,6 +112,8 @@
     load_e.wait()
     send_e.start()
 
+    load_w1.wait()
+    load_w2.wait()
     pre = nn(q_ref[...], w1_ref[...])
     act[...] = pre
     hid[...] = jnp.maximum(pre, 0.0).astype(BF16)
@@ -162,10 +168,11 @@
         return settle, drain
 
     quarter = half // 2
+    place = {block: (t, c) for t in range(len(ORDER)) for c, block in enumerate(blocks_of(t))}
 
     def loc_x(slot, h, part):
-        k = POS[slot]
-        return xg.at[k, h] if part is None else xg.at[k, h, pl.ds(part * quarter, quarter)]
+        t, c = place[(POS[slot], h)]
+        return xg.at[t, c] if part is None else xg.at[t, c, pl.ds(part * quarter, quarter)]
 
     x_arrived, x_forward, x_drain = tree(loc_x, ag_s, ag_r)
     x_forward((0, 0))
@@ -185,8 +192,7 @@
         return pl.ds(pl.multiple_of(i * tile, tile), tile)
 
     def x_of(t):
-        (k0, h0), (k1, h1) = blocks_of(t)
-        return jnp.concatenate([xg[k0, h0], xg[k1, h1]], axis=0)
+        return xg[t].reshape(rows, dim)
 
     def turned(i):
         return lax.rem(i + core * (ntile // 2), ntile)
@@ -247,10 +253,10 @@
                 stat_copy(k, h).start()
 
     def bc_copy(k, h):
-        return remote(bco.at[h], bci.at[POS[back(ORDER[k])], h], bc_s.at[k, h], bc_r.at[POS[back(ORDER[k])], h], dev(*owner_off(h, ORDER[k])))
+        return remote(bco.at[h], bci.at[place[(POS[back(ORDER[k])], h)]], bc_s.at[k, h], bc_r.at[POS[back(ORDER[k])], h], dev(*owner_off(h, ORDER[k])))
 
     def bc_recv(k, h):
-        return remote(bco.at[h], bci.at[k, h], bc_s.at[k, h], bc_r.at[k, h], me)
+        return remote(bco.at[h], bci.at[place[(k, h)]], bc_s.at[k, h], bc_r.at[k, h], me)
 
     def combine(h):
         sti[0, h] = sto[0, h]
@@ -332,8 +338,8 @@
     lo_x = dim // 2
 
     def acc_x(slot, h, part):
-        k = POS[slot]
-        return part_x.at[k, h] if part is None else part_x.at[k, h, pl.ds(part * lo_x, lo_x)]
+        t, c = place[(POS[slot], h)]
+        return part_x.at[t, c] if part is None else part_x.at[t, c, pl.ds(part * lo_x, lo_x)]
 
     def box_x(i, h):
         return rbf.at[FULL.index(i), h] if i in FULL else rbp.at[PART.index(i), h]
@@ -353,9 +359,9 @@
 
     def soften(z_ref, g_ref, o, s, i):
         slot = lax.rem(s * ntile + i, ring)
-        (k0, h0), (k1, h1) = blocks_of(backward_step(s))
-        lse = jnp.concatenate([bci[k0, h0, 0:1, :], bci[k1, h1, 0:1, :]], axis=1)
-        lab = jnp.concatenate([bci[k0, h0, 1:2, :], bci[k1, h1, 1:2, :]], axis=1).astype(jnp.int32) - (first_item + i * tile)
+        t = backward_step(s)
+        lse = jnp.concatenate([bci[t, 0, 0:1, :], bci[t, 1, 0:1, :]], axis=1)
+        lab = jnp.concatenate([bci[t, 0, 1:2, :], bci[t, 1, 1:2, :]], axis=1).astype(jnp.int32) - (first_item + i * tile)
         lab = lab - lax.broadcasted_iota(jnp.int32, (8, rows), 0)
         acc = jnp.zeros((8, rows), F32)
         for r in chunks():
@@ -370,9 +376,10 @@
 
     def spread(g_ref, s, i):
         dx = nn(ets[i], g_ref[...])
+        t = backward_step(s)
         for r in range(0, dim, part):
-            for c, (k, h) in enumerate(blocks_of(backward_step(s))):
-                part_x[k, h, r:r + part, :] += dx[r:r + part, c * half:(c + 1) * half]
+            for c in range(2):
+                part_x[t, c, r:r + part, :] += dx[r:r + part, c * half:(c + 1) * half]
 
     def settle_step(t):
         for k, h in reversed(blocks_of(t)):
@@ -402,7 +409,7 @@
                     @pl.when(s == k)
                     def _(k=k):
                         settle_step(order2[k - 1])
-                        if k == 2:
+                        if k == 1:
                             combine(1)
                         if k == SOLO - 1:
                             broadcast_in(1)
@@ -543,6 +550,10 @@
     def de_send(j):
         return remote(de.at[j], der.at[j], de_s.at[j], de_r.at[j], partner)
 
+    def de_store(j):
+        at = pl.ds(pl.multiple_of(j * crows, crows), crows)
+        return pltpu.make_async_copy(de_out.at[at], de_hbm.at[at], deo_sem.at[j])
+
     def chunk(j):
         g_in(j).wait()
         slot = lax.rem(j, 2)
@@ -575,6 +586,11 @@
             de_send(hchunk - 1).start()
 
         own = j - hchunk
+
+        @pl.when(own > 0)
+        def _():
+            de_store(own - 1).start()
+
         grad = chunk(j)
         de_send(own).wait_recv()
         de_out[pl.ds(pl.multiple_of(own * crows, crows), crows), :] = (grad + der[own]).astype(BF16)
@@ -583,6 +599,7 @@
         def _():
             g_in(j + 2).start()
 
+    de_store(hchunk - 1).start()
     pair_copy(0).start()
     for k in range(1, chips):
         lb_recv(k).wait_recv()
@@ -611,6 +628,7 @@
     g_drain()
     for j in range(hchunk):
         de_send(j).wait_send()
+        de_store(j).wait()
     for k in range(chips):
         pair_copy(k).wait_send()
         for h in range(2):
@@ -655,8 +673,8 @@
                 jax.ShapeDtypeStruct((1,), F32),
                 jax.ShapeDtypeStruct((chips, 2 * items, rows), BF16),
             ],
-            in_specs=[vspec] * 4 + [aspec] * 2,
-            out_specs=[vspec, aspec, aspec, pl.BlockSpec(memory_space=pltpu.SMEM), aspec],
+            in_specs=[vspec] * 2 + [aspec] * 4,
+            out_specs=[aspec, aspec, aspec, pl.BlockSpec(memory_space=pltpu.SMEM), aspec],
             scratch_shapes=[
                 vm((chips, 2, half, dim), BF16),
                 vm((2 * items, dim), BF16),
@@ -691,7 +709,10 @@
                 vm((ring, tile, rows), BF16),
                 vm((2, chips, crows, rows), BF16),
                 vm((hidden, rows), BF16),
-                dma((2,)), dma((ring,)), dma((2,)), dma((2, chips, 2)), dma((6,)), dma((6,)),
+                vm((dim, hidden), BF16),
+                vm((hidden, dim), BF16),
+                vm((items, dim), BF16),
+                dma((4,)), dma((items // crows,)), dma((ring,)), dma((2,)), dma((2, chips, 2)), dma((6,)), dma((6,)),
                 dma((items // crows,)), dma((items // crows,)), dma((chips,)), dma((chips,)), dma((chips, 2)), dma((chips, 2)),
                 dma((NMSG, 2)), dma((NMSG, 2)),
                 dma((chips, 2)), dma((chips, 2)),
@@ -702,7 +723,7 @@
                 dma((chips,)), dma((chips,)),
             ],
             compiler_params=pltpu.CompilerParams(collective_id=0, has_side_effects=True, vmem_limit_bytes=67_043_328),
-        )(queries, w_first, w_second, lab, catalogue, lq)
+        )(queries, lab, w_first, w_second, catalogue, lq)
         return loss, de, dw1, dw2
 
     row_spec = P(("dp", "tp"), None)

time: 167 us -> 163 us (0.976)
  Pallas kernels: 159 us -> 155 us
    pallas_call x1, Pallas kernels: 159 us -> 155 us  [local_step(): pl.pallas_call(functools.partial(kernel, (n, total_rows, tile)), out_shap...]
where the time goes in v7:
time: 163 us
  Pallas kernels  155 us (95%)
  local copies, waits for them, and re-layouts  5.52 us (3%)
  between operations  2.4 us (1%)
    pallas_call x1, Pallas kernels, local_step(): pl.pallas_call(functools.partial(kernel, (n, total_rows, tile)), out_shap...  155 us
    unnamed x7, local copies, waits for them, and re-layouts  5.52 us

profile of v7, /device:TPU:97, one launch (start us, length us, event | category | flops | bytes accessed | tf_op | source)
XLA Modules:
  0.0 162.7 jit_solution(11472838387893176642)
XLA Ops:
  0.6 154.7 %shard_map.93 = (bf16[2048,384]{1,0:T(8,128)(2,1)}, bf16[384,1536]{1,0:T(8,128)(2,1)}, bf16[1536,384]{1,0:T(8,128)(2,1)}, f32[1]{0:T(128)}, bf16[16,4096,256]{2,1,0:T(8,128)(2,1)}) custom-call(bf16[256,384]{1,0:T(8,128)(2,1)} %q_ref.1, s32[1,256]{1,0:T(1,128)} %bitcast.3, bf16[384,1536]{1,0:T(8,128)(2,1)} %w1_hbm.1, bf16[1536,384]{1,0:T(8,128)(2,1)} %w2_hbm.1, ...), custom_call_target="tpu_custom_call" | custom-call | tf_op jit(solution)/shard_map/pallas_call | solution.py:667
  156.0 0.0 copy-start.1
  156.0 2.8 %copy.15 = bf16[2048,384]{1,0:T(8,128)(2,1)} copy(bf16[2048,384]{1,0:T(8,128)(2,1)} %get-tuple-element.17) | data formatting | bytes 3145728
  158.8 0.0 copy-done.1
  158.8 0.0 copy-start
  158.8 1.0 copy.16
  159.8 0.7 copy-done
  160.5 1.0 copy.17
Async XLA Ops:
  156.0 2.8 %copy-start.1 = (bf16[384,1536]{1,0:T(8,128)(2,1)S(1)}, bf16[384,1536]{1,0:T(8,128)(2,1)}, u32[]{:S(2)}) copy-start(bf16[384,1536]{1,0:T(8,128)(2,1)} %get-tuple-element.18) | copy-start | bytes 3538948
  158.8 1.7 %copy-start = (bf16[1536,384]{1,0:T(8,128)(2,1)S(1)}, bf16[1536,384]{1,0:T(8,128)(2,1)}, u32[]{:S(2)}) copy-start(bf16[1536,384]{1,0:T(8,128)(2,1)} %get-tuple-element.19) | copy-start | bytes 3538948
